TPU v7x, 32 devices: a whole 2x2x4 slice. The times are simulated.
32 devices in a mesh: sub: 8 (over z, x), rng: 4 (over y, core).
Axes of the slice: x: 2, y: 2, z: 4, core: 2. Of those that a mesh axis runs over, the one named last changes fastest.
Arguments:
- echoes: bfloat16 [2, 4, 1024, 2048], P(None, None, 'sub', 'rng'), may hold values from -6 to 6
- steering: bfloat16 [2, 256, 256], replicated, may hold values from -0.25 to 0.25
- sub_map: int32 [8], replicated, may hold values from 0 to 7, each once
- band_offset: int32 [8, 3, 2, 256], P('sub'), may hold values from 0 to 248, as said below
- interp_weight: bfloat16 [8, 3, 2, 8, 256], P('sub'), may hold values from -1.5 to 1.5
- range_frac: float32 [8, 3, 2, 256], P('sub'), may hold values from 0 to 1
- phase_rate: float32 [8, 3, 2, 256], P('sub'), may hold values from -40 to 40
Outputs:
- image: bfloat16 [2, 4096, 2048], P(None, 'rng', 'sub')
Inputs may be any that keep to these rules, and one draw needn't show every extreme that they name: `sub_map`: each number appears once. `band_offset`: an entry for section i and segment s lies in h * 128 to (h + 1) * 128 - 8, where h is bit s of i.
All inputs are finite; a program needn't handle non-finite values.
Results may differ from a plain program's by a relative error of at most 0.0062.
Values may be sent and summed in bfloat16 or wider, within the bound.
No kernel may reach another device: no remote copies, remote signals or barrier semaphores. Data moves between devices by JAX's collectives and lax.ppermute only.
A program may use at most 64 MiB of HBM per device.

v0:
```python
import functools

import jax
import jax.numpy as jnp
from jax import lax
from jax.experimental import pallas as pl
from jax.experimental.pallas import tpu as pltpu
from jax.sharding import PartitionSpec as P


HALO = 8
KINDS = 6
MIB = 1 << 20
WHOLE = pl.BlockSpec(memory_space=pltpu.VMEM)
SCALARS = pl.BlockSpec(memory_space=pltpu.SMEM)
FAR = pl.BlockSpec(memory_space=pltpu.HBM)


def exchanged(block, axis, mask):
    count = lax.axis_size(axis)
    return lax.ppermute(block, axis, [(source, source ^ mask) for source in range(count)])


def params(mib):
    return pltpu.CompilerParams(vmem_limit_bytes=mib * MIB)


def cost(flops):
    return pl.CostEstimate(flops=flops, bytes_accessed=MIB, transcendentals=0)


def product(left, right):
    return (
        left[0] * right[0] - left[1] * right[1],
        left[0] * right[1] + left[1] * right[0],
    )


def pack_rows(terms, taps):
    return -(-(terms * (taps + KINDS)) // 8) * 8


def cut_kernel(slabs, segments, taps, half, echoes, offset, weight, fraction, rate, *refs):
    slices, packs = refs[:slabs], refs[slabs : slabs + 2]
    held, semaphores, small = refs[slabs + 2 : slabs + 6], refs[slabs + 6], refs[slabs + 7]
    group = 1 << segments
    member = lax.axis_index("sub") & (group - 1)
    slab = lax.axis_index("rng")
    loads = [
        pltpu.make_async_copy(source, target, small.at[index])
        for index, (source, target) in enumerate(zip((offset, weight, fraction, rate), held))
    ]
    copies = []
    for mask in range(slabs - 1, -1, -1):
        for c in range(2):
            copies.append(
                pltpu.make_async_copy(
                    echoes.at[c, slab ^ mask], slices[mask].at[c], semaphores.at[mask, c]
                )
            )
    for copy in loads + copies:
        copy.start()
    for copy in loads:
        copy.wait()
    offset, weight, fraction, rate = held
    angles = weight.shape[-1]
    for pack, chosen in ((packs[0], range(segments - 1)), (packs[1], (segments - 1,))):
        kinds = [[] for _ in range(KINDS)]
        terms = 2 * len(chosen)
        for index, segment in enumerate(chosen):
            base = ((member >> segment) & 1) * half
            kinds[0].append((offset[0, segment] - base).astype(jnp.float32))
            slot = 1
            for source, count in ((fraction, 2), (rate, 3)):
                rest = source[0, segment]
                for _ in range(count):
                    part = rest.astype(jnp.bfloat16).astype(jnp.float32)
                    kinds[slot].append(part)
                    rest = rest - part
                    slot += 1
            for child in range(2):
                term = index * 2 + child
                pack[term * taps : (term + 1) * taps, :] = weight[0, segment, child]
        rows = [piece for kind in kinds for piece in kind]
        padding = pack_rows(terms, taps) - terms * (taps + KINDS)
        if padding:
            rows.append(jnp.zeros((padding, angles), jnp.float32))
        pack[terms * taps :, :] = jnp.concatenate(rows, axis=0).astype(jnp.bfloat16)
    for copy in copies:
        copy.wait()


def table_kernel(members, terms, masks, taps, half, rows, lines, range_rows, total_range, *refs):
    steps = len(masks[0]) if masks else 0
    swapped = steps - 1 if masks else 0
    own, mine, theirs = refs[0], refs[1 : 1 + steps], refs[1 + steps : 1 + steps + swapped]
    bands, waves, weights, raw, dense = refs[1 + steps + swapped :]
    angles = bands.shape[-1]
    member = lax.axis_index("sub") & (members - 1)
    slab = lax.axis_index("rng")

    def fill(piece, section):
        values = piece[...].astype(jnp.float32)
        for term in range(terms):
            weights[section, term] = values[term * taps : (term + 1) * taps]
        start = terms * taps
        kind = [values[start + k * terms : start + (k + 1) * terms] for k in range(KINDS)]
        raw[section, 0] = kind[0]
        raw[section, 1] = kind[1] + kind[2]
        raw[section, 2] = kind[3] + kind[4] + kind[5]

    if masks:
        core = slab & 1
        fill(own, member)
        for received, holder in ((mine, core), (theirs, 1 - core)):
            for step, piece in enumerate(received):
                fill(piece, member ^ jnp.where(holder == 0, masks[0][step], masks[1][step]))
        first_row, row_step = slab * range_rows + member * rows, 0
    else:
        for section in range(members):
            fill(own, section)
        first_row, row_step = slab * range_rows, rows

    for start in range(0, members * terms, 8):
        place = slice(start, start + 8)
        sections = range(start // terms, (start + 8) // terms)

        def keep(kind, value):
            for part in range(angles // 128):
                dense[kind, part, place] = value[:, part * 128 : (part + 1) * 128]

        given = [
            jnp.concatenate([raw[section, kind] for section in sections], axis=0)
            for kind in range(3)
        ]
        keep(0, given[0])
        keep(1, given[1])
        rate = given[2]
        number = start + lax.broadcasted_iota(jnp.int32, (8, angles), 0)
        first = first_row + (number // terms) * row_step
        angle = first.astype(jnp.float32) / float(total_range) * rate
        keep(3, jnp.cos(angle))
        keep(4, jnp.sin(angle))
        angle = rate / float(total_range)
        turn = jnp.cos(angle), jnp.sin(angle)
        for power in range(5):
            keep(5 + 2 * power, turn[0])
            keep(6 + 2 * power, turn[1])
            turn = product(turn, turn)

    sub_rows = lax.broadcasted_iota(jnp.int32, (8, 128), 0)

    def entry(index, carry):
        section, term = index // terms, index % terms
        for part in range(angles // 128):
            lanes = pl.ds(part * 128, 128)

            def row(kind):
                return dense[kind, part, pl.ds(index, 1), :]

            def bands_of():
                weight = weights[section, term, :, lanes]
                offset = row(0).astype(jnp.int32)
                fraction = row(1)
                tap = sub_rows - offset
                block_of = -(tap >> 3)
                picked = jnp.take_along_axis(weight, tap & 7, axis=0)
                near, far = picked * (1.0 - fraction), picked * fraction
                for block in range(half // 16):
                    hits = [block_of == 2 * block + step for step in range(2)]
                    for source, base in ((near, 0), (far, half)):
                        pair = [jnp.where(hit, source, 0.0) for hit in hits]
                        place = slice(base + block * 16, base + (block + 1) * 16)
                        bands[section, term, place, lanes] = jnp.concatenate(pair, axis=0).astype(
                            jnp.bfloat16
                        )

            if masks:
                bands_of()
            else:
                pl.when(section == 0)(bands_of)
            wave = tuple(jnp.broadcast_to(row(3 + c), (8, 128)) for c in range(2))
            for power in range(3):
                chosen = (sub_rows >> power) & 1 == 1
                wave = product(
                    wave,
                    (
                        jnp.where(chosen, row(5 + 2 * power), 1.0),
                        jnp.where(chosen, row(6 + 2 * power), 0.0),
                    ),
                )
            eight, sixteen = (row(11), row(12)), (row(13), row(14))
            chain = [wave, product(wave, eight)]
            for block in range(lines // 8):
                wave = chain[block % 2]
                for c in range(2):
                    waves[section, term, c, block * 8 : (block + 1) * 8, lanes] = wave[c]
                chain[block % 2] = product(wave, sixteen)
        return carry

    lax.fori_loop(0, members * terms, entry, 0)


def formed(steering, re_parts, im_parts):
    rows = jnp.concatenate(re_parts + im_parts, axis=0)
    count = rows.shape[0] // 2
    by_real, by_imag = [
        lax.dot_general(
            rows, steering[c], (((1,), (1,)), ((), ())), preferred_element_type=jnp.float32
        )
        for c in range(2)
    ]
    return by_real[:count] - by_imag[count:], by_imag[:count] + by_real[count:]


def place_of(sub_map, group, slabs, slab, index):
    if slabs == 1:
        return index
    per_slab = group // slabs
    block = (slab ^ (index // per_slab)) * per_slab + index % per_slab
    place = 0
    for section in range(group):
        place = jnp.where(sub_map[section] == block, section, place)
    return place


def form_kernel(group, pulse_count, sources, first, count, sub_map, *refs):
    blocks, steering, image = refs[:sources], refs[sources], refs[sources + 1]
    half = image.shape[-1]
    per_source = group // sources
    slab = lax.axis_index("rng")
    for source in range(sources):
        for start in range(0, per_source, 2):
            pieces = range(start, min(start + 2, per_source))
            parts = [
                [
                    blocks[source][
                        c, first : first + count, piece * pulse_count : (piece + 1) * pulse_count
                    ]
                    for piece in pieces
                ]
                for c in range(2)
            ]
            values = formed(steering, *parts)
            for index, piece in enumerate(pieces):
                target = place_of(sub_map, group, sources, slab, source * per_source + piece)
                for c in range(2):
                    value = values[c][index * count : (index + 1) * count]
                    for window in range(2):
                        image[target, c, window] = value[:, window * half : (window + 1) * half]


def turned(values, block, first):
    total = None
    for value, wave in values:
        part = value[block * 16 : block * 16 + 8], value[block * 16 + 8 : block * 16 + 16]
        start = first + block * 8
        turn = tuple(wave[c, start : start + 8] for c in range(2))
        term = product(turn, part)
        total = term if total is None else (total[0] + term[0], total[1] + term[1])
    return total


def contracted(rows_of, lines, matrix):
    pieces = []
    for block in range(lines // 8):
        sides = []
        for start in (block * 8, block * 8 + 1):
            both = [rows_of(c, start) for c in range(2)]
            sides.append(jnp.concatenate(both, axis=0).astype(jnp.bfloat16))
        pieces.append(jnp.concatenate(sides, axis=1))
    return jnp.dot(jnp.concatenate(pieces, axis=0), matrix, preferred_element_type=jnp.float32)


def merge_kernel(group, segments, chunk, rows, pulse_count, sources, *refs):
    near = group // 2
    if chunk == 0:
        image, bands, waves = refs[:3]
        refs = refs[3:]
    else:
        sub_map, image, edge, steering, bands, waves = refs[:6]
        kept, edges, refs = refs[6 : 6 + near], refs[6 + near + group], refs[6 + near :]
        refs = refs[:group] + refs[group + 1 :]
    outs, stores = refs[:group], refs[group:]
    half = image.shape[-1]
    member = lax.axis_index("sub") & (group - 1)
    per_source = group // sources

    if chunk == 1:
        below = lax.axis_index("rng")
        if sources > 1:
            below = jnp.minimum(below + jnp.where(member == group - 1, 1, 0), sources - 1)
        parts = [[], []]
        for source in range(sources):
            for piece in range(per_source):
                columns = slice(piece * pulse_count, (piece + 1) * pulse_count)
                for c in range(2):
                    parts[c].append(edge[source, c, :, columns])
        values = formed(steering, *parts)
        for index in range(group):
            target = place_of(sub_map, group, sources, below, index)
            for c in range(2):
                value = values[c][index * HALO : (index + 1) * HALO]
                for window in range(2):
                    edges[target, c, window, 0:HALO] = value[:, window * half : (window + 1) * half]
                    edges[target, c, window, HALO:] = jnp.zeros((8, half), jnp.float32)

    def rows_of(segment, section, window, c, start):
        if segment > 0:
            return stores[segment - 1][section, c, window, start : start + 8]
        if chunk == 0 or start + 8 <= rows:
            return image[section, c, window, start : start + 8]
        if start >= rows:
            return edges[section, c, window, start - rows : start - rows + 8]
        return jnp.concatenate(
            [
                image[section, c, window, start:rows],
                edges[section, c, window, 0 : start + 8 - rows],
            ],
            axis=0,
        )

    for segment in range(segments - 1):

        def step(section, carry, segment=segment):
            low = section & ~(1 << segment)
            window = (section >> segment) & 1
            values = []
            for child in range(2):
                source, term = low | (child << segment), segment * 2 + child
                reader = functools.partial(rows_of, segment, source, window)
                value = contracted(reader, rows + 8, bands[section, term])
                values.append((value, waves.at[section, term]))
            for block in range(rows // 8 + 1):
                for c, total in enumerate(turned(values, block, chunk * rows)):
                    for side in range(2):
                        stores[segment][section, c, side, block * 8 : block * 8 + 8] = total[
                            :, side * half : (side + 1) * half
                        ]
            for c in range(2):
                for side in range(2):
                    stores[segment][section, c, side, rows + 8 :] = jnp.zeros(
                        (8, half), jnp.float32
                    )
            return carry

        lax.fori_loop(0, group, step, 0, unroll=4)

    last = stores[segments - 2]
    size = 4 * rows + 8
    for mask in range(group):
        section = member ^ mask
        low = section & ~(1 << (segments - 1))
        window = (section >> (segments - 1)) & 1
        base = 0
        if chunk == 1 and mask < near:
            outs[mask][0:size] = kept[mask][...]
            base = size
        extra = []
        for child in range(2):
            for c in range(2):
                start = base + (child * 2 + c) * rows
                source = last.at[low | (child << (segments - 1)), c, window]
                outs[mask][start : start + rows] = source[0:rows].astype(jnp.bfloat16)
                extra.append(source[rows : rows + 1])
        extra.append(jnp.zeros((4, half), jnp.float32))
        outs[mask][base + 4 * rows : base + size] = jnp.concatenate(extra, axis=0).astype(
            jnp.bfloat16
        )


def final_kernel(jobs, count, group, rows, first, *refs):
    parts, (bands, waves) = refs[:count], refs[count : count + 2]
    result, store, mine, semaphores = refs[count + (2 if first else 3) :]
    half = store.shape[-1]
    member = lax.axis_index("sub") & (group - 1)
    copies = []
    for index, (source, base, mask, chunk) in enumerate(jobs):
        part = parts[source]
        extra = part[base + 4 * rows : base + 4 * rows + 8].astype(jnp.float32)
        for side in range(4):
            start = base + side * rows
            store[index, side, 0:rows] = part[start : start + rows].astype(jnp.float32)
            store[index, side, rows:] = jnp.broadcast_to(extra[side : side + 1], (8, half))
        values = []
        for child in range(2):

            def rows_of(c, start, index=index, child=child):
                return store[index, child * 2 + c, start : start + 8]

            value = contracted(rows_of, rows, bands[0, child])
            values.append((value, waves.at[member ^ mask, child]))
        held = None
        for block in range(rows // 8):
            totals = turned(values, block, chunk * rows)
            if block % 2 == 0:
                held = totals
                continue
            for c in range(2):
                mine[index, c, block * 8 - 8 : block * 8 + 8] = jnp.concatenate(
                    [held[c], totals[c]], axis=0
                ).astype(jnp.bfloat16)
        start = pl.multiple_of(((member ^ mask) * 2 + chunk) * rows, rows)
        for c in range(2):
            copy = pltpu.make_async_copy(
                mine.at[index, c], result.at[c, pl.ds(start, rows)], semaphores.at[index, c]
            )
            copy.start()
            copies.append(copy)
    for copy in copies:
        copy.wait()


def send_order(group):
    far, near = list(range(group - 1, group // 2 - 1, -1)), list(range(group // 2 - 1, 0, -1))
    order = [(mask, 0) for mask in far] + [(mask, 1) for mask in far[:2]]
    return order + [(mask, None) for mask in near] + [(mask, 1) for mask in far[2:]]


def on_device(echoes, steering, sub_map, band_offset, interp_weight, range_frac, phase_rate):
    slabs = lax.axis_size("rng")
    subs = lax.axis_size("sub")
    segments, taps = interp_weight.shape[1], interp_weight.shape[3]
    group = 1 << segments
    groups = subs // group
    angles, pulse_count = steering.shape[1], steering.shape[2]
    half = angles // 2
    slab = lax.axis_index("rng")
    range_rows = echoes.shape[2] * subs
    rows = range_rows // group
    early, late = 2 * (segments - 1), 2

    cut = (2,) + echoes.shape[2:]
    tables_in = (band_offset, interp_weight, range_frac, phase_rate)
    *quarters, early_pack, late_pack = pl.pallas_call(
        functools.partial(cut_kernel, slabs, segments, taps, half),
        out_shape=[pltpu.VMEM(cut, jnp.bfloat16)] * slabs
        + [pltpu.VMEM((pack_rows(terms, taps), angles), jnp.bfloat16) for terms in (early, late)],
        in_specs=[FAR] * 5,
        out_specs=[WHOLE] * (slabs + 2),
        scratch_shapes=[pltpu.VMEM(value.shape, value.dtype) for value in tables_in]
        + [pltpu.SemaphoreType.DMA((slabs, 2)), pltpu.SemaphoreType.DMA((4,))],
        compiler_params=params(2),
        cost_estimate=cost(1_000_000_000),
        name="cut",
    )(*[pltpu.with_memory_space_constraint(value, pltpu.HBM) for value in (echoes,) + tables_in])

    received = [quarters[0]] + [None] * (slabs - 1)
    for mask in range(slabs - 1, 0, -1):
        received[mask] = exchanged(quarters[mask], "rng", mask)

    masks = list(range(group - 1, 1, -1))
    masks = (masks[0::2] + [1], masks[1::2] + [1])
    mine, theirs = [], []
    for step in range(len(masks[0])):
        route = []
        for s in range(subs):
            for q in range(slabs):
                route.append((s * slabs + q, (s ^ masks[q & 1][step]) * slabs + q))
        mine.append(lax.ppermute(early_pack, ("sub", "rng"), route))
    for piece in mine[:-1]:
        theirs.append(exchanged(piece, "rng", 1))

    if groups == 1:
        blocks = received
    else:
        ordered = jnp.zeros((slabs,) + received[0].shape, received[0].dtype)
        for mask, block in enumerate(received):
            ordered = lax.dynamic_update_index_in_dim(ordered, block, slab ^ mask, 0)
        every = jnp.moveaxis(ordered, 0, 2).reshape(2, -1, subs, pulse_count)
        every = jnp.take(every, sub_map, axis=2)
        every = lax.ppermute(
            every,
            "sub",
            [(old, (old % groups) * group + old // groups) for old in range(subs)],
        ).reshape(2, -1, groups, group * pulse_count)
        lanes = [[g * group + m for g in range(groups)] for m in range(group)]
        every = lax.all_to_all(every, "sub", 2, 1, axis_index_groups=lanes, tiled=True)
        blocks = [every.reshape(2, rows, group * pulse_count)]

    edge_rows = jnp.stack([block[:, :HALO] for block in blocks])
    route = []
    for number in range(subs):
        for q in range(slabs):
            if number % group > 0:
                route.append((number * slabs + q, (number - 1) * slabs + q))
            elif q > 0:
                route.append((number * slabs + q, (number + group - 1) * slabs + q - 1))
    edge = lax.ppermute(edge_rows, ("sub", "rng"), route)

    def tables(terms, sources, held, lines, arrays):
        return pl.pallas_call(
            functools.partial(
                table_kernel,
                group,
                terms,
                sources,
                taps,
                half,
                rows,
                lines,
                range_rows,
                slabs * range_rows,
            ),
            out_shape=(
                jax.ShapeDtypeStruct((held, terms, angles, angles), jnp.bfloat16),
                jax.ShapeDtypeStruct((group, terms, 2, lines, angles), jnp.float32),
            ),
            in_specs=[WHOLE] * len(arrays),
            out_specs=(WHOLE, WHOLE),
            scratch_shapes=[
                pltpu.VMEM((group, terms, taps, angles), jnp.float32),
                pltpu.VMEM((group, 3, terms, angles), jnp.float32),
                pltpu.VMEM((15, angles // 128, group * terms, 128), jnp.float32),
            ],
            compiler_params=params(4),
            cost_estimate=cost(2_000_000_000),
        )(*arrays)

    bands, waves = tables(early, masks, group, rows + 8, [early_pack, *mine, *theirs])

    chunk_rows = rows // 2
    near = group // 2

    def form(first, count):
        return pl.pallas_call(
            functools.partial(form_kernel, group, pulse_count, len(blocks), first, count),
            out_shape=jax.ShapeDtypeStruct((group, 2, 2, count, half), jnp.float32),
            in_specs=[SCALARS] + [WHOLE] * (len(blocks) + 1),
            out_specs=WHOLE,
            compiler_params=params(6),
            cost_estimate=cost(1_000_000_000),
        )(sub_map, *blocks, steering)

    piece = 4 * chunk_rows + 8

    def merge(chunk, arrays, sizes):
        edges = [pltpu.VMEM((group, 2, 2, 16, half), jnp.float32)] if chunk == 1 else []
        return pl.pallas_call(
            functools.partial(
                merge_kernel, group, segments, chunk, chunk_rows, pulse_count, len(blocks)
            ),
            out_shape=[jax.ShapeDtypeStruct((size, half), jnp.bfloat16) for size in sizes],
            in_specs=([SCALARS] if chunk == 1 else []) + [WHOLE] * (len(arrays) - chunk),
            out_specs=[WHOLE] * group,
            scratch_shapes=edges
            + [pltpu.VMEM((group, 2, 2, chunk_rows + 16, half), jnp.float32)] * (segments - 1),
            compiler_params=params(8),
            cost_estimate=cost(4_000_000_000),
        )(*arrays)

    order = send_order(group)
    arrived = {}

    def send(mask, chunk, value):
        arrived[mask, chunk] = exchanged(value, "sub", mask)

    upper = merge(0, [form(0, chunk_rows + 16), bands, waves], [piece] * group)
    for mask in range(near, group):
        send(mask, 0, upper[mask])
    lower = merge(
        1,
        [sub_map, form(chunk_rows, chunk_rows), edge, steering, bands, waves]
        + list(upper[:near]),
        [2 * piece] * near + [piece] * near,
    )
    for mask in range(near, group):
        send(mask, 1, lower[mask])
    for mask in range(1, near):
        send(mask, None, lower[mask])
    arrived[0, None] = lower[0]

    last_bands, last_waves = tables(late, None, 1, rows, [late_pack])
    result = None
    turns = [
        [(0, None)] + order[:near],
        order[near:-2],
        order[-2:-1],
        order[-1:],
    ]
    for chosen in turns:
        count = len(chosen)
        jobs = []
        for source, (mask, chunk) in enumerate(chosen):
            if chunk is None:
                jobs += [(source, 0, mask, 0), (source, piece, mask, 1)]
            else:
                jobs.append((source, 0, mask, chunk))
        previous = [] if result is None else [result]
        result = pl.pallas_call(
            functools.partial(final_kernel, jobs, count, group, chunk_rows, result is None),
            out_shape=jax.ShapeDtypeStruct((2, range_rows, angles), jnp.bfloat16),
            in_specs=[WHOLE] * (count + 2) + [FAR] * len(previous),
            out_specs=FAR,
            scratch_shapes=[
                pltpu.VMEM((len(jobs), 4, chunk_rows + 8, half), jnp.float32),
                pltpu.VMEM((len(jobs), 2, chunk_rows, angles), jnp.bfloat16),
                pltpu.SemaphoreType.DMA((len(jobs), 2)),
            ],
            input_output_aliases={count + 2: 0} if previous else {},
            compiler_params=params(6),
            cost_estimate=cost(1_000_000_000),
            name="final",
        )(*[arrived[key] for key in chosen], last_bands, last_waves, *previous)
    return result


def solution(mesh):
    in_specs = (
        P(None, None, "sub", "rng"),
        P(),
        P(),
        P("sub", None, None, None),
        P("sub", None, None, None, None),
        P("sub", None, None, None),
        P("sub", None, None, None),
    )
    return jax.shard_map(
        on_device, mesh=mesh, in_specs=in_specs, out_specs=P(None, "rng", "sub"), check_vma=False
    )
```

profile of v0, /device:TPU:0, one launch (start us, length us, event | category | flops | bytes accessed | tf_op | source)
XLA Modules:
  0.0 62.6 jit_solution(4275558428440973617)
XLA Ops:
  0.0 1.4 %cut.1 = (bf16[2,128,512]{2,1,0:T(8,128)(2,1)S(1)}, bf16[2,128,512]{2,1,0:T(8,128)(2,1)S(1)}, bf16[2,128,512]{2,1,0:T(8,128)(2,1)S(1)}, bf16[2,128,512]{2,1,0:T(...) custom-call(bf16[2,4,128,512]{3,2,1,0:T(8,128)(2,1)} %echoes.1, s32[1,3,2,256]{3,2,1,0:T(2,128)} %offset.1, ...), custom_call_target="tpu_custom_call" | custom-call | flops 1000000000 | bytes 1048576 | tf_op jit(solution)/shard_map/cut/pallas_call | solution.py:435
  1.5 4.0 %collective-permute-start.6 = (bf16[56,256]{1,0:T(8,128)(2,1)S(1)}, bf16[56,256]{1,0:T(8,128)(2,1)S(1)}, u32[]{:S(2)}, u32[]{:S(2)}) collective-permute-start(bf16[56,256]{1,0:T(8,128)(2,1)S(1)} %get-tuple-element.35.refs_0_), channel_id=1, source_target_pairs={{0,12},{1,9},{2,14},{3,11},{4,8},{5,13},{6,10},{7,15},{8,4},{9,1},... | collective-permute-start | bytes 86024 | tf_op jit(solution)/shard_map/ppermute | solution.py:460
  5.5 2.4 %collective-permute-start.4 = (bf16[56,256]{1,0:T(8,128)(2,1)S(1)}, bf16[56,256]{1,0:T(8,128)(2,1)S(1)}, u32[]{:S(2)}, u32[]{:S(2)}) collective-permute-start(bf16[56,256]{1,0:T(8,128)(2,1)S(1)} %get-tuple-element.35.refs_0_), channel_id=1, source_target_pairs={{0,28},{1,25},{2,30},{3,27},{4,24},{5,29},{6,26},{7,31},{8,20},{9,... | collective-permute-start | bytes 86024 | tf_op jit(solution)/shard_map/ppermute | solution.py:460
  8.3 1.2 %collective-permute-start.7 = (bf16[56,256]{1,0:T(8,128)(2,1)S(1)}, bf16[56,256]{1,0:T(8,128)(2,1)S(1)}, u32[]{:S(2)}, u32[]{:S(2)}) collective-permute-start(bf16[56,256]{1,0:T(8,128)(2,1)S(1)} %get-tuple-element.35.refs_0_), channel_id=1, source_target_pairs={{0,4},{1,5},{2,6},{3,7},{4,0},{5,1},{6,2},{7,3},{8,12},{9,13},{10,... | collective-permute-start | bytes 86024 | tf_op jit(solution)/shard_map/ppermute | solution.py:460
  9.6 1.6 %collective-permute-start.10 = (bf16[56,256]{1,0:T(8,128)(2,1)S(1)}, bf16[56,256]{1,0:T(8,128)(2,1)S(1)}, u32[]{:S(2)}, u32[]{:S(2)}) collective-permute-start(bf16[56,256]{1,0:T(8,128)(2,1)S(1)} %collective-permute-done.6.refs_3_), channel_id=1, source_target_pairs={{0,1},{1,0},{2,3},{3,2},{4,5},{5,4},{6,7},{7,6},{8,9},{9,8},{10,11... | collective-permute-start | bytes 86024 | tf_op jit(solution)/shard_map/ppermute | solution.py:21
  12.1 1.8 %collective-permute-done.5.refs_2_ = bf16[56,256]{1,0:T(8,128)(2,1)S(1)} collective-permute-done((bf16[56,256]{1,0:T(8,128)(2,1)S(1)}, bf16[56,256]{1,0:T(8,128)(2,1)S(1)}, u32[]{:S(2)}, u32[]{:S(2)}) %collective-permute-start.5) | collective-permute-done | bytes 28704 | tf_op jit(solution)/shard_map/ppermute | solution.py:460
  14.4 1.5 %collective-permute-start.1 = (bf16[2,128,512]{2,1,0:T(8,128)(2,1)S(1)}, bf16[2,128,512]{2,1,0:T(8,128)(2,1)S(1)}, u32[]{:S(2)}, u32[]{:S(2)}) collective-permute-start(bf16[2,128,512]{2,1,0:T(8,128)(2,1)S(1)} %get-tuple-element.33), channel_id=1, source_target_pairs={{0,2},{1,3},{2,0},{3,1},{4,6},{5,7},{6,4},{7,5},{8,10},{9,11},{10,... | collective-permute-start | bytes 786440 | tf_op jit(solution)/shard_map/ppermute | solution.py:21
  16.0 2.7 %shard_map.74 = (bf16[8,4,256,256]{3,2,1,0:T(8,128)(2,1)S(1)}, f32[8,4,2,136,256]{4,3,2,1,0:T(8,128)S(1)}) custom-call(bf16[56,256]{1,0:T(8,128)(2,1)S(1)} %get-tuple-element.35.refs_0_, bf16[56,256]{1,0:T(8,128)(2,1)S(1)} %collective-permute-done.4.refs_1_, bf16[56,256]{1,0:T(8,128)(2,1)S(1)} %collective-permute-done.5.refs_2_, ...), custom_call_target="tpu_custom_call" | custom-call | flops 2000000000 | bytes 1048576 | tf_op jit(solution)/shard_map/pallas_call | solution.py:492
  18.7 5.1 %collective-permute-done.1.refs_2_ = bf16[2,128,512]{2,1,0:T(8,128)(2,1)S(1)} collective-permute-done((bf16[2,128,512]{2,1,0:T(8,128)(2,1)S(1)}, bf16[2,128,512]{2,1,0:T(8,128)(2,1)S(1)}, u32[]{:S(2)}, u32[]{:S(2)}) %collective-permute-start.1) | collective-permute-done | bytes 262176 | tf_op jit(solution)/shard_map/ppermute | solution.py:21
  23.8 1.3 %collective-permute-start.3 = (bf16[4,2,8,512]{3,2,1,0:T(8,128)(2,1)S(1)}, bf16[4,2,8,512]{3,2,1,0:T(8,128)(2,1)S(1)}, u32[]{:S(2)}, u32[]{:S(2)}) collective-permute-start(bf16[4,2,8,512]{3,2,1,0:T(8,128)(2,1)S(1)} %pad_maximum_fusion), channel_id=1, source_target_pairs={{1,28},{2,29},{3,30},{4,0},{5,1},{6,2},{7,3},{8,4},{9,5},{10,6},{1... | collective-permute-start | bytes 196616 | tf_op jit(solution)/shard_map/ppermute | solution.py:489
  26.2 1.5 %shard_map.76 = (bf16[264,128]{1,0:T(8,128)(2,1)S(1)}, bf16[264,128]{1,0:T(8,128)(2,1)S(1)}, bf16[264,128]{1,0:T(8,128)(2,1)S(1)}, bf16[264,128]{1,0:T(8,128)(2,...) custom-call(f32[8,2,2,80,128]{4,3,2,1,0:T(8,128)S(1)} %shard_map.75., ...), custom_call_target="tpu_custom_call" | custom-call | flops 4000000000 | bytes 1048576 | tf_op jit(solution)/shard_map/pallas_call | solution.py:539
  27.8 5.1 %collective-permute-start.18 = (bf16[264,128]{1,0:T(8,128)(2,1)S(1)}, bf16[264,128]{1,0:T(8,128)(2,1)S(1)}, u32[]{:S(2)}, u32[]{:S(2)}) collective-permute-start(bf16[264,128]{1,0:T(8,128)(2,1)S(1)} %get-tuple-element.53), channel_id=1, source_target_pairs={{0,28},{4,24},{8,20},{12,16},{16,12},{20,8},{24,4},{28,0},{1,29},{... | collective-permute-start | bytes 202760 | tf_op jit(solution)/shard_map/ppermute | solution.py:21
  33.7 1.8 %collective-permute-start.20 = (bf16[264,128]{1,0:T(8,128)(2,1)S(1)}, bf16[264,128]{1,0:T(8,128)(2,1)S(1)}, u32[]{:S(2)}, u32[]{:S(2)}) collective-permute-start(bf16[264,128]{1,0:T(8,128)(2,1)S(1)} %get-tuple-element.55), channel_id=1, source_target_pairs={{0,20},{4,16},{8,28},{12,24},{16,4},{20,0},{24,12},{28,8},{1,21},{... | collective-permute-start | bytes 202760 | tf_op jit(solution)/shard_map/ppermute | solution.py:21
  35.5 1.9 %collective-permute-start.21 = (bf16[264,128]{1,0:T(8,128)(2,1)S(1)}, bf16[264,128]{1,0:T(8,128)(2,1)S(1)}, u32[]{:S(2)}, u32[]{:S(2)}) collective-permute-start(bf16[264,128]{1,0:T(8,128)(2,1)S(1)} %get-tuple-element.56), channel_id=1, source_target_pairs={{0,16},{4,20},{8,24},{12,28},{16,0},{20,4},{24,8},{28,12},{1,17},{... | collective-permute-start | bytes 202760 | tf_op jit(solution)/shard_map/ppermute | solution.py:21
  38.5 2.3 %shard_map.77 = (bf16[528,128]{1,0:T(8,128)(2,1)S(1)}, bf16[528,128]{1,0:T(8,128)(2,1)S(1)}, bf16[528,128]{1,0:T(8,128)(2,1)S(1)}, bf16[528,128]{1,0:T(8,128)(2,...) custom-call(s32[8]{0:T(128)S(1)} %copy-done.1, ...), custom_call_target="tpu_custom_call" | custom-call | flops 4000000000 | bytes 1048576 | tf_op jit(solution)/shard_map/pallas_call | solution.py:539
  40.8 1.5 %collective-permute-start.15 = (bf16[528,128]{1,0:T(8,128)(2,1)S(1)}, bf16[528,128]{1,0:T(8,128)(2,1)S(1)}, u32[]{:S(2)}, u32[]{:S(2)}) collective-permute-start(bf16[528,128]{1,0:T(8,128)(2,1)S(1)} %get-tuple-element.49), channel_id=1, source_target_pairs={{0,12},{4,8},{8,4},{12,0},{16,28},{20,24},{24,20},{28,16},{1,13},{... | collective-permute-start | bytes 405512 | tf_op jit(solution)/shard_map/ppermute | solution.py:21
  43.0 1.3 %collective-permute-start.17 = (bf16[528,128]{1,0:T(8,128)(2,1)S(1)}, bf16[528,128]{1,0:T(8,128)(2,1)S(1)}, u32[]{:S(2)}, u32[]{:S(2)}) collective-permute-start(bf16[528,128]{1,0:T(8,128)(2,1)S(1)} %get-tuple-element.51), channel_id=1, source_target_pairs={{0,4},{4,0},{8,12},{12,8},{16,20},{20,16},{24,28},{28,24},{1,5},{5... | collective-permute-start | bytes 405512 | tf_op jit(solution)/shard_map/ppermute | solution.py:21
  44.4 1.3 %shard_map.78 = (bf16[1,2,256,256]{3,2,1,0:T(8,128)(2,1)S(1)}, f32[8,2,2,128,256]{4,3,2,1,0:T(8,128)S(1)}) custom-call(bf16[32,256]{1,0:T(8,128)(2,1)S(1)} %get-tuple-element.43.refs_0_), custom_call_target="tpu_custom_call" | custom-call | flops 2000000000 | bytes 1048576 | tf_op jit(solution)/shard_map/pallas_call | solution.py:492
  45.7 3.3 %collective-permute-start.13 = (bf16[264,128]{1,0:T(8,128)(2,1)S(1)}, bf16[264,128]{1,0:T(8,128)(2,1)S(1)}, u32[]{:S(2)}, u32[]{:S(2)}) collective-permute-start(bf16[264,128]{1,0:T(8,128)(2,1)S(1)} %get-tuple-element.47), channel_id=1, source_target_pairs={{0,28},{4,24},{8,20},{12,16},{16,12},{20,8},{24,4},{28,0},{1,29},{... | collective-permute-start | bytes 202760 | tf_op jit(solution)/shard_map/ppermute | solution.py:21
  49.7 1.2 %final.4.refs_7_ = bf16[2,1024,256]{2,1,0:T(8,128)(2,1)} custom-call(bf16[528,128]{1,0:T(8,128)(2,1)S(1)} %get-tuple-element.52.refs_0_, bf16[264,128]{1,0:T(8,128)(2,1)S(1)} %collective-permute-done.18.refs_1_, bf16[264,128]{1,0:T(8,128)(2,1)S(1)} %collective-permute-done.19.refs_2_, bf16[264,128]{1,0:T(8,128)(2,1)S(1)} %collective-permute-done.20.refs_3_, ...), custom_call_target="tpu_custom_call" | custom-call | flops 1000000000 | bytes 1048576 | tf_op jit(solution)/shard_map/final/pallas_call | solution.py:590
  50.9 2.7 %collective-permute-done.13.refs_0_ = bf16[264,128]{1,0:T(8,128)(2,1)S(1)} collective-permute-done((bf16[264,128]{1,0:T(8,128)(2,1)S(1)}, bf16[264,128]{1,0:T(8,128)(2,1)S(1)}, u32[]{:S(2)}, u32[]{:S(2)}) %collective-permute-start.13) | collective-permute-done | bytes 67616 | tf_op jit(solution)/shard_map/ppermute | solution.py:21
  53.8 1.9 %collective-permute-done.14.refs_1_ = bf16[264,128]{1,0:T(8,128)(2,1)S(1)} collective-permute-done((bf16[264,128]{1,0:T(8,128)(2,1)S(1)}, bf16[264,128]{1,0:T(8,128)(2,1)S(1)}, u32[]{:S(2)}, u32[]{:S(2)}) %collective-permute-start.14) | collective-permute-done | bytes 67616 | tf_op jit(solution)/shard_map/ppermute | solution.py:21
  56.6 1.3 %final.5.refs_3_ = bf16[2,1024,256]{2,1,0:T(8,128)(2,1)} custom-call(bf16[264,128]{1,0:T(8,128)(2,1)S(1)} %collective-permute-done.13.refs_0_, bf16[264,128]{1,0:T(8,128)(2,1)S(1)} %collective-permute-done.14.refs_1_, bf16[528,128]{1,0:T(8,128)(2,1)S(1)} %collective-permute-done.15.refs_2_, ...), custom_call_target="tpu_custom_call", output_to_operand_aliasing={{}: (7, {})} | custom-call | flops 1000000000 | bytes 1048576 | tf_op jit(solution)/shard_map/final/pallas_call | solution.py:590
  57.9 3.0 %collective-permute-done.12.refs_0_ = bf16[264,128]{1,0:T(8,128)(2,1)S(1)} collective-permute-done((bf16[264,128]{1,0:T(8,128)(2,1)S(1)}, bf16[264,128]{1,0:T(8,128)(2,1)S(1)}, u32[]{:S(2)}, u32[]{:S(2)}) %collective-permute-start.12) | collective-permute-done | bytes 67616 | tf_op jit(solution)/shard_map/ppermute | solution.py:21
  (40 shorter events, 9.0 us)
Async XLA Ops:
  1.4 23.7 %copy-start = (bf16[2,256,256]{2,1,0:T(8,128)(2,1)S(1)}, bf16[2,256,256]{2,1,0:T(8,128)(2,1)}, u32[]{:S(2)}) copy-start(bf16[2,256,256]{2,1,0:T(8,128)(2,1)} %refs_3_.1) | copy-start | bytes 786436
  1.4 23.7 %copy-start.1 = (s32[8]{0:T(128)S(1)}, s32[8]{0:T(128)}, u32[]{:S(2)}) copy-start(s32[8]{0:T(128)} %refs_0_.1) | copy-start | bytes 100
  1.5 8.1 %collective-permute-start.6 = (bf16[56,256]{1,0:T(8,128)(2,1)S(1)}, bf16[56,256]{1,0:T(8,128)(2,1)S(1)}, u32[]{:S(2)}, u32[]{:S(2)}) collective-permute-start(bf16[56,256]{1,0:T(8,128)(2,1)S(1)} %get-tuple-element.35.refs_0_), channel_id=1, source_target_pairs={{0,12},{1,9},{2,14},{3,11},{4,8},{5,13},{6,10},{7,15},{8,4},{9,1},... | collective-permute-start | bytes 86024 | tf_op jit(solution)/shard_map/ppermute | solution.py:460
  5.5 6.6 %collective-permute-start.4 = (bf16[56,256]{1,0:T(8,128)(2,1)S(1)}, bf16[56,256]{1,0:T(8,128)(2,1)S(1)}, u32[]{:S(2)}, u32[]{:S(2)}) collective-permute-start(bf16[56,256]{1,0:T(8,128)(2,1)S(1)} %get-tuple-element.35.refs_0_), channel_id=1, source_target_pairs={{0,28},{1,25},{2,30},{3,27},{4,24},{5,29},{6,26},{7,31},{8,20},{9,... | collective-permute-start | bytes 86024 | tf_op jit(solution)/shard_map/ppermute | solution.py:460
  7.9 6.0 %collective-permute-start.5 = (bf16[56,256]{1,0:T(8,128)(2,1)S(1)}, bf16[56,256]{1,0:T(8,128)(2,1)S(1)}, u32[]{:S(2)}, u32[]{:S(2)}) collective-permute-start(bf16[56,256]{1,0:T(8,128)(2,1)S(1)} %get-tuple-element.35.refs_0_), channel_id=1, source_target_pairs={{0,20},{1,17},{2,22},{3,19},{4,16},{5,21},{6,18},{7,23},{8,28},{9,... | collective-permute-start | bytes 86024 | tf_op jit(solution)/shard_map/ppermute | solution.py:460
  8.3 5.6 %collective-permute-start.7 = (bf16[56,256]{1,0:T(8,128)(2,1)S(1)}, bf16[56,256]{1,0:T(8,128)(2,1)S(1)}, u32[]{:S(2)}, u32[]{:S(2)}) collective-permute-start(bf16[56,256]{1,0:T(8,128)(2,1)S(1)} %get-tuple-element.35.refs_0_), channel_id=1, source_target_pairs={{0,4},{1,5},{2,6},{3,7},{4,0},{5,1},{6,2},{7,3},{8,12},{9,13},{10,... | collective-permute-start | bytes 86024 | tf_op jit(solution)/shard_map/ppermute | solution.py:460
  9.6 9.1 %collective-permute-start.2 = (bf16[2,128,512]{2,1,0:T(8,128)(2,1)S(1)}, bf16[2,128,512]{2,1,0:T(8,128)(2,1)S(1)}, u32[]{:S(2)}, u32[]{:S(2)}) collective-permute-start(bf16[2,128,512]{2,1,0:T(8,128)(2,1)S(1)} %get-tuple-element.34), channel_id=1, source_target_pairs={{0,3},{1,2},{2,1},{3,0},{4,7},{5,6},{6,5},{7,4},{8,11},{9,10},{10,... | collective-permute-start | bytes 786440 | tf_op jit(solution)/shard_map/ppermute | solution.py:21
  9.6 4.9 %collective-permute-start.10 = (bf16[56,256]{1,0:T(8,128)(2,1)S(1)}, bf16[56,256]{1,0:T(8,128)(2,1)S(1)}, u32[]{:S(2)}, u32[]{:S(2)}) collective-permute-start(bf16[56,256]{1,0:T(8,128)(2,1)S(1)} %collective-permute-done.6.refs_3_), channel_id=1, source_target_pairs={{0,1},{1,0},{2,3},{3,2},{4,5},{5,4},{6,7},{7,6},{8,9},{9,8},{10,11... | collective-permute-start | bytes 86024 | tf_op jit(solution)/shard_map/ppermute | solution.py:21
  12.1 3.9 %collective-permute-start.8 = (bf16[56,256]{1,0:T(8,128)(2,1)S(1)}, bf16[56,256]{1,0:T(8,128)(2,1)S(1)}, u32[]{:S(2)}, u32[]{:S(2)}) collective-permute-start(bf16[56,256]{1,0:T(8,128)(2,1)S(1)} %collective-permute-done.4.refs_1_), channel_id=1, source_target_pairs={{0,1},{1,0},{2,3},{3,2},{4,5},{5,4},{6,7},{7,6},{8,9},{9,8},{10,11... | collective-permute-start | bytes 86024 | tf_op jit(solution)/shard_map/ppermute | solution.py:21
  13.9 2.0 %collective-permute-start.9 = (bf16[56,256]{1,0:T(8,128)(2,1)S(1)}, bf16[56,256]{1,0:T(8,128)(2,1)S(1)}, u32[]{:S(2)}, u32[]{:S(2)}) collective-permute-start(bf16[56,256]{1,0:T(8,128)(2,1)S(1)} %collective-permute-done.5.refs_2_), channel_id=1, source_target_pairs={{0,1},{1,0},{2,3},{3,2},{4,5},{5,4},{6,7},{7,6},{8,9},{9,8},{10,11... | collective-permute-start | bytes 86024 | tf_op jit(solution)/shard_map/ppermute | solution.py:21
  13.9 9.9 %collective-permute-start = (bf16[2,128,512]{2,1,0:T(8,128)(2,1)S(1)}, bf16[2,128,512]{2,1,0:T(8,128)(2,1)S(1)}, u32[]{:S(2)}, u32[]{:S(2)}) collective-permute-start(bf16[2,128,512]{2,1,0:T(8,128)(2,1)S(1)} %get-tuple-element.32), channel_id=1, source_target_pairs={{0,1},{1,0},{2,3},{3,2},{4,5},{5,4},{6,7},{7,6},{8,9},{9,8},{10,11... | collective-permute-start | bytes 786440 | tf_op jit(solution)/shard_map/ppermute | solution.py:21
  14.4 9.3 %collective-permute-start.1 = (bf16[2,128,512]{2,1,0:T(8,128)(2,1)S(1)}, bf16[2,128,512]{2,1,0:T(8,128)(2,1)S(1)}, u32[]{:S(2)}, u32[]{:S(2)}) collective-permute-start(bf16[2,128,512]{2,1,0:T(8,128)(2,1)S(1)} %get-tuple-element.33), channel_id=1, source_target_pairs={{0,2},{1,3},{2,0},{3,1},{4,6},{5,7},{6,4},{7,5},{8,10},{9,11},{10,... | collective-permute-start | bytes 786440 | tf_op jit(solution)/shard_map/ppermute | solution.py:21
  23.8 14.7 %collective-permute-start.3 = (bf16[4,2,8,512]{3,2,1,0:T(8,128)(2,1)S(1)}, bf16[4,2,8,512]{3,2,1,0:T(8,128)(2,1)S(1)}, u32[]{:S(2)}, u32[]{:S(2)}) collective-permute-start(bf16[4,2,8,512]{3,2,1,0:T(8,128)(2,1)S(1)} %pad_maximum_fusion), channel_id=1, source_target_pairs={{1,28},{2,29},{3,30},{4,0},{5,1},{6,2},{7,3},{8,4},{9,5},{10,6},{1... | collective-permute-start | bytes 196616 | tf_op jit(solution)/shard_map/ppermute | solution.py:489
  27.8 14.6 %collective-permute-start.18 = (bf16[264,128]{1,0:T(8,128)(2,1)S(1)}, bf16[264,128]{1,0:T(8,128)(2,1)S(1)}, u32[]{:S(2)}, u32[]{:S(2)}) collective-permute-start(bf16[264,128]{1,0:T(8,128)(2,1)S(1)} %get-tuple-element.53), channel_id=1, source_target_pairs={{0,28},{4,24},{8,20},{12,16},{16,12},{20,8},{24,4},{28,0},{1,29},{... | collective-permute-start | bytes 202760 | tf_op jit(solution)/shard_map/ppermute | solution.py:21
  32.8 10.2 %collective-permute-start.19 = (bf16[264,128]{1,0:T(8,128)(2,1)S(1)}, bf16[264,128]{1,0:T(8,128)(2,1)S(1)}, u32[]{:S(2)}, u32[]{:S(2)}) collective-permute-start(bf16[264,128]{1,0:T(8,128)(2,1)S(1)} %get-tuple-element.54), channel_id=1, source_target_pairs={{0,24},{4,28},{8,16},{12,20},{16,8},{20,12},{24,0},{28,4},{1,25},{... | collective-permute-start | bytes 202760 | tf_op jit(solution)/shard_map/ppermute | solution.py:21
  33.7 11.9 %collective-permute-start.20 = (bf16[264,128]{1,0:T(8,128)(2,1)S(1)}, bf16[264,128]{1,0:T(8,128)(2,1)S(1)}, u32[]{:S(2)}, u32[]{:S(2)}) collective-permute-start(bf16[264,128]{1,0:T(8,128)(2,1)S(1)} %get-tuple-element.55), channel_id=1, source_target_pairs={{0,20},{4,16},{8,28},{12,24},{16,4},{20,0},{24,12},{28,8},{1,21},{... | collective-permute-start | bytes 202760 | tf_op jit(solution)/shard_map/ppermute | solution.py:21
  35.5 13.4 %collective-permute-start.21 = (bf16[264,128]{1,0:T(8,128)(2,1)S(1)}, bf16[264,128]{1,0:T(8,128)(2,1)S(1)}, u32[]{:S(2)}, u32[]{:S(2)}) collective-permute-start(bf16[264,128]{1,0:T(8,128)(2,1)S(1)} %get-tuple-element.56), channel_id=1, source_target_pairs={{0,16},{4,20},{8,24},{12,28},{16,0},{20,4},{24,8},{28,12},{1,17},{... | collective-permute-start | bytes 202760 | tf_op jit(solution)/shard_map/ppermute | solution.py:21
  40.8 15.8 %collective-permute-start.15 = (bf16[528,128]{1,0:T(8,128)(2,1)S(1)}, bf16[528,128]{1,0:T(8,128)(2,1)S(1)}, u32[]{:S(2)}, u32[]{:S(2)}) collective-permute-start(bf16[528,128]{1,0:T(8,128)(2,1)S(1)} %get-tuple-element.49), channel_id=1, source_target_pairs={{0,12},{4,8},{8,4},{12,0},{16,28},{20,24},{24,20},{28,16},{1,13},{... | collective-permute-start | bytes 405512 | tf_op jit(solution)/shard_map/ppermute | solution.py:21
  42.3 14.2 %collective-permute-start.16 = (bf16[528,128]{1,0:T(8,128)(2,1)S(1)}, bf16[528,128]{1,0:T(8,128)(2,1)S(1)}, u32[]{:S(2)}, u32[]{:S(2)}) collective-permute-start(bf16[528,128]{1,0:T(8,128)(2,1)S(1)} %get-tuple-element.50), channel_id=1, source_target_pairs={{0,8},{4,12},{8,0},{12,4},{16,24},{20,28},{24,16},{28,20},{1,9},{5... | collective-permute-start | bytes 405512 | tf_op jit(solution)/shard_map/ppermute | solution.py:21
  43.0 13.6 %collective-permute-start.17 = (bf16[528,128]{1,0:T(8,128)(2,1)S(1)}, bf16[528,128]{1,0:T(8,128)(2,1)S(1)}, u32[]{:S(2)}, u32[]{:S(2)}) collective-permute-start(bf16[528,128]{1,0:T(8,128)(2,1)S(1)} %get-tuple-element.51), channel_id=1, source_target_pairs={{0,4},{4,0},{8,12},{12,8},{16,20},{20,16},{24,28},{28,24},{1,5},{5... | collective-permute-start | bytes 405512 | tf_op jit(solution)/shard_map/ppermute | solution.py:21
  45.7 7.9 %collective-permute-start.13 = (bf16[264,128]{1,0:T(8,128)(2,1)S(1)}, bf16[264,128]{1,0:T(8,128)(2,1)S(1)}, u32[]{:S(2)}, u32[]{:S(2)}) collective-permute-start(bf16[264,128]{1,0:T(8,128)(2,1)S(1)} %get-tuple-element.47), channel_id=1, source_target_pairs={{0,28},{4,24},{8,20},{12,16},{16,12},{20,8},{24,4},{28,0},{1,29},{... | collective-permute-start | bytes 202760 | tf_op jit(solution)/shard_map/ppermute | solution.py:21
  49.0 6.8 %collective-permute-start.14 = (bf16[264,128]{1,0:T(8,128)(2,1)S(1)}, bf16[264,128]{1,0:T(8,128)(2,1)S(1)}, u32[]{:S(2)}, u32[]{:S(2)}) collective-permute-start(bf16[264,128]{1,0:T(8,128)(2,1)S(1)} %get-tuple-element.48), channel_id=1, source_target_pairs={{0,24},{4,28},{8,16},{12,20},{16,8},{20,12},{24,0},{28,4},{1,25},{... | collective-permute-start | bytes 202760 | tf_op jit(solution)/shard_map/ppermute | solution.py:21
  53.5 7.4 %collective-permute-start.12 = (bf16[264,128]{1,0:T(8,128)(2,1)S(1)}, bf16[264,128]{1,0:T(8,128)(2,1)S(1)}, u32[]{:S(2)}, u32[]{:S(2)}) collective-permute-start(bf16[264,128]{1,0:T(8,128)(2,1)S(1)} %get-tuple-element.46), channel_id=1, source_target_pairs={{0,20},{4,16},{8,28},{12,24},{16,4},{20,0},{24,12},{28,8},{1,21},{... | collective-permute-start | bytes 202760 | tf_op jit(solution)/shard_map/ppermute | solution.py:21
  55.8 6.0 %collective-permute-start.11 = (bf16[264,128]{1,0:T(8,128)(2,1)S(1)}, bf16[264,128]{1,0:T(8,128)(2,1)S(1)}, u32[]{:S(2)}, u32[]{:S(2)}) collective-permute-start(bf16[264,128]{1,0:T(8,128)(2,1)S(1)} %get-tuple-element.42), channel_id=1, source_target_pairs={{0,16},{4,20},{8,24},{12,28},{16,0},{20,4},{24,8},{28,12},{1,17},{... | collective-permute-start | bytes 202760 | tf_op jit(solution)/shard_map/ppermute | solution.py:21
where the time goes:
time: 62.8 us; the launch traced here: 62.6 us
  starting transfers between devices  31.4 us (50%)
  Pallas kernels  15.5 us (25%)
  waiting for transfers between devices  15.5 us (25%)
    ppermute x17, starting transfers between devices, exchanged(): lax.ppermute(block, axis, [(source, source ^ mask) for source in range(co...  22 us
    ppermute x17, waiting for transfers between devices, exchanged(): lax.ppermute(block, axis, [(source, source ^ mask) for source in range(co...  12.7 us
    ppermute x4, starting transfers between devices, on_device(): mine.append(lax.ppermute(early_pack, ('sub', 'rng'), route))  8.1 us
    pallas_call x4, Pallas kernels, on_device(): pl.pallas_call(functools.partial(final_kernel, jobs, count, group, chunk_...  4.19 us
    pallas_call x2, Pallas kernels, tables(): pl.pallas_call(functools.partial(table_kernel, group, terms, sources, tap...  3.98 us
    pallas_call x2, Pallas kernels, merge(): pl.pallas_call(functools.partial(merge_kernel, group, segments, chunk, ch...  3.82 us
    ppermute x4, waiting for transfers between devices, on_device(): mine.append(lax.ppermute(early_pack, ('sub', 'rng'), route))  2.73 us
    pallas_call x2, Pallas kernels, form(): pl.pallas_call(functools.partial(form_kernel, group, pulse_count, len(blo...  2.12 us
  transfers between devices with their start and end apart: 22, of which 6 were waited for; matrix products, arithmetic and copies ran while one was open for 0% of the time, Pallas kernels for 21%

commit v1 on v0

--- a/solution.py
+++ b/solution.py
@@ -272,15 +272,14 @@
     return jnp.dot(jnp.concatenate(pieces, axis=0), matrix, preferred_element_type=jnp.float32)
 
 
-def merge_kernel(group, segments, chunk, rows, pulse_count, sources, *refs):
-    near = group // 2
+def merge_kernel(group, segments, chunk, first, rows, whole, pulse_count, sources, *refs):
     if chunk == 0:
         image, bands, waves = refs[:3]
         refs = refs[3:]
     else:
         sub_map, image, edge, steering, bands, waves = refs[:6]
-        kept, edges, refs = refs[6 : 6 + near], refs[6 + near + group], refs[6 + near :]
-        refs = refs[:group] + refs[group + 1 :]
+        kept, refs = dict(zip(whole, refs[6:])), refs[6 + len(whole) :]
+        edges, refs = refs[group], refs[:group] + refs[group + 1 :]
     outs, stores = refs[:group], refs[group:]
     half = image.shape[-1]
     member = lax.axis_index("sub") & (group - 1)
@@ -332,7 +331,7 @@
                 value = contracted(reader, rows + 8, bands[section, term])
                 values.append((value, waves.at[section, term]))
             for block in range(rows // 8 + 1):
-                for c, total in enumerate(turned(values, block, chunk * rows)):
+                for c, total in enumerate(turned(values, block, first)):
                     for side in range(2):
                         stores[segment][section, c, side, block * 8 : block * 8 + 8] = total[
                             :, side * half : (side + 1) * half
@@ -353,9 +352,9 @@
         low = section & ~(1 << (segments - 1))
         window = (section >> (segments - 1)) & 1
         base = 0
-        if chunk == 1 and mask < near:
-            outs[mask][0:size] = kept[mask][...]
-            base = size
+        if chunk == 1 and mask in whole:
+            base = kept[mask].shape[0]
+            outs[mask][0:base] = kept[mask][...]
         extra = []
         for child in range(2):
             for c in range(2):
@@ -369,19 +368,19 @@
         )
 
 
-def final_kernel(jobs, count, group, rows, first, *refs):
+def final_kernel(jobs, count, group, block_rows, fresh, *refs):
     parts, (bands, waves) = refs[:count], refs[count : count + 2]
-    result, store, mine, semaphores = refs[count + (2 if first else 3) :]
+    result, store, mine, semaphores = refs[count + (2 if fresh else 3) :]
     half = store.shape[-1]
     member = lax.axis_index("sub") & (group - 1)
     copies = []
-    for index, (source, base, mask, chunk) in enumerate(jobs):
+    for index, (source, base, mask, first, rows) in enumerate(jobs):
         part = parts[source]
         extra = part[base + 4 * rows : base + 4 * rows + 8].astype(jnp.float32)
         for side in range(4):
             start = base + side * rows
             store[index, side, 0:rows] = part[start : start + rows].astype(jnp.float32)
-            store[index, side, rows:] = jnp.broadcast_to(extra[side : side + 1], (8, half))
+            store[index, side, rows : rows + 8] = jnp.broadcast_to(extra[side : side + 1], (8, half))
         values = []
         for child in range(2):
 
@@ -392,7 +391,7 @@
             values.append((value, waves.at[member ^ mask, child]))
         held = None
         for block in range(rows // 8):
-            totals = turned(values, block, chunk * rows)
+            totals = turned(values, block, first)
             if block % 2 == 0:
                 held = totals
                 continue
@@ -400,10 +399,10 @@
                 mine[index, c, block * 8 - 8 : block * 8 + 8] = jnp.concatenate(
                     [held[c], totals[c]], axis=0
                 ).astype(jnp.bfloat16)
-        start = pl.multiple_of(((member ^ mask) * 2 + chunk) * rows, rows)
+        start = pl.multiple_of((member ^ mask) * block_rows + first, 16)
         for c in range(2):
             copy = pltpu.make_async_copy(
-                mine.at[index, c], result.at[c, pl.ds(start, rows)], semaphores.at[index, c]
+                mine.at[index, c, 0:rows], result.at[c, pl.ds(start, rows)], semaphores.at[index, c]
             )
             copy.start()
             copies.append(copy)
@@ -413,8 +412,9 @@
 
 def send_order(group):
     far, near = list(range(group - 1, group // 2 - 1, -1)), list(range(group // 2 - 1, 0, -1))
-    order = [(mask, 0) for mask in far] + [(mask, 1) for mask in far[:2]]
-    return order + [(mask, None) for mask in near] + [(mask, 1) for mask in far[2:]]
+    upper = [(mask, 0) for mask in far[:2]]
+    rest = [(mask, None) for mask in far[2:3] + near + far[3:]]
+    return upper, rest + [(mask, 1) for mask in far[:2]]
 
 
 def on_device(echoes, steering, sub_map, band_offset, interp_weight, range_frac, phase_rate):
@@ -519,8 +519,12 @@
 
     bands, waves = tables(early, masks, group, rows + 8, [early_pack, *mine, *theirs])
 
-    chunk_rows = rows // 2
-    near = group // 2
+    cut_row = -(-rows * 5 // 8 // 16) * 16
+    bounds = ((0, cut_row), (cut_row, rows - cut_row))
+    pieces = [4 * count + 8 for _, count in bounds]
+    upper_order, lower_order = send_order(group)
+    split = [mask for mask, _ in upper_order]
+    whole_masks = [mask for mask in range(group) if mask not in split]
 
     def form(first, count):
         return pl.pallas_call(
@@ -532,69 +536,67 @@
             cost_estimate=cost(1_000_000_000),
         )(sub_map, *blocks, steering)
 
-    piece = 4 * chunk_rows + 8
-
     def merge(chunk, arrays, sizes):
+        first, count = bounds[chunk]
         edges = [pltpu.VMEM((group, 2, 2, 16, half), jnp.float32)] if chunk == 1 else []
         return pl.pallas_call(
             functools.partial(
-                merge_kernel, group, segments, chunk, chunk_rows, pulse_count, len(blocks)
+                merge_kernel,
+                group,
+                segments,
+                chunk,
+                first,
+                count,
+                whole_masks,
+                pulse_count,
+                len(blocks),
             ),
             out_shape=[jax.ShapeDtypeStruct((size, half), jnp.bfloat16) for size in sizes],
             in_specs=([SCALARS] if chunk == 1 else []) + [WHOLE] * (len(arrays) - chunk),
             out_specs=[WHOLE] * group,
             scratch_shapes=edges
-            + [pltpu.VMEM((group, 2, 2, chunk_rows + 16, half), jnp.float32)] * (segments - 1),
+            + [pltpu.VMEM((group, 2, 2, count + 16, half), jnp.float32)] * (segments - 1),
             compiler_params=params(8),
             cost_estimate=cost(4_000_000_000),
         )(*arrays)
 
-    order = send_order(group)
     arrived = {}
 
     def send(mask, chunk, value):
         arrived[mask, chunk] = exchanged(value, "sub", mask)
 
-    upper = merge(0, [form(0, chunk_rows + 16), bands, waves], [piece] * group)
-    for mask in range(near, group):
-        send(mask, 0, upper[mask])
+    upper = merge(0, [form(0, cut_row + 16), bands, waves], pieces[:1] * group)
+    for mask, chunk in upper_order:
+        send(mask, chunk, upper[mask])
     lower = merge(
         1,
-        [sub_map, form(chunk_rows, chunk_rows), edge, steering, bands, waves]
-        + list(upper[:near]),
-        [2 * piece] * near + [piece] * near,
+        [sub_map, form(*bounds[1]), edge, steering, bands, waves]
+        + [upper[mask] for mask in whole_masks],
+        [sum(pieces) if mask in whole_masks else pieces[1] for mask in range(group)],
     )
-    for mask in range(near, group):
-        send(mask, 1, lower[mask])
-    for mask in range(1, near):
-        send(mask, None, lower[mask])
+    for mask, chunk in lower_order:
+        send(mask, chunk, lower[mask])
     arrived[0, None] = lower[0]
 
     last_bands, last_waves = tables(late, None, 1, rows, [late_pack])
     result = None
-    turns = [
-        [(0, None)] + order[:near],
-        order[near:-2],
-        order[-2:-1],
-        order[-1:],
-    ]
+    turns = [[(0, None)] + upper_order, lower_order[:-3]] + [[key] for key in lower_order[-3:]]
     for chosen in turns:
         count = len(chosen)
         jobs = []
         for source, (mask, chunk) in enumerate(chosen):
-            if chunk is None:
-                jobs += [(source, 0, mask, 0), (source, piece, mask, 1)]
-            else:
-                jobs.append((source, 0, mask, chunk))
+            for part in (0, 1) if chunk is None else (chunk,):
+                base = pieces[0] if chunk is None and part == 1 else 0
+                jobs.append((source, base, mask) + bounds[part])
         previous = [] if result is None else [result]
         result = pl.pallas_call(
-            functools.partial(final_kernel, jobs, count, group, chunk_rows, result is None),
+            functools.partial(final_kernel, jobs, count, group, rows, result is None),
             out_shape=jax.ShapeDtypeStruct((2, range_rows, angles), jnp.bfloat16),
             in_specs=[WHOLE] * (count + 2) + [FAR] * len(previous),
             out_specs=FAR,
             scratch_shapes=[
-                pltpu.VMEM((len(jobs), 4, chunk_rows + 8, half), jnp.float32),
-                pltpu.VMEM((len(jobs), 2, chunk_rows, angles), jnp.bfloat16),
+                pltpu.VMEM((len(jobs), 4, cut_row + 8, half), jnp.float32),
+                pltpu.VMEM((len(jobs), 2, cut_row, angles), jnp.bfloat16),
                 pltpu.SemaphoreType.DMA((len(jobs), 2)),
             ],
             input_output_aliases={count + 2: 0} if previous else {},

time: 62.8 us -> 59.6 us (0.949)
  waiting for transfers between devices: 15.5 us -> 12.1 us
  Pallas kernels: 15.5 us -> 16.3 us
    ppermute x17 -> x15, waiting for transfers between devices: 12.7 us -> 9.39 us  [exchanged(): lax.ppermute(block, axis, [(source, source ^ mask) for source in range(co...]
    pallas_call x6 -> x7, Pallas kernels: 8.01 us -> 8.65 us  [the longest x5 4.93 us: on_device(): pl.pallas_call(functools.partial(final_kernel, jobs, count, group, rows,...]
    ppermute x17 -> x15, starting transfers between devices: 22 us -> 21.4 us  [exchanged(): lax.ppermute(block, axis, [(source, source ^ mask) for source in range(co...]
  transfers between devices with their start and end apart: 22 -> 20, of which waited for: 6 -> 5; matrix products, arithmetic and copies ran while one was open for 0% -> 0% of each run, Pallas kernels for 21% -> 24%
where the time goes in v1:
time: 59.6 us; the launch traced here: 59.4 us
  starting transfers between devices  30.8 us (52%)
  Pallas kernels  16.3 us (27%)
  waiting for transfers between devices  12.1 us (20%)
    ppermute x15, starting transfers between devices, exchanged(): lax.ppermute(block, axis, [(source, source ^ mask) for source in range(co...  21.4 us
    ppermute x15, waiting for transfers between devices, exchanged(): lax.ppermute(block, axis, [(source, source ^ mask) for source in range(co...  9.39 us
    ppermute x4, starting transfers between devices, on_device(): mine.append(lax.ppermute(early_pack, ('sub', 'rng'), route))  8.1 us
    pallas_call x5, Pallas kernels, on_device(): pl.pallas_call(functools.partial(final_kernel, jobs, count, group, rows,...  4.93 us
    pallas_call x2, Pallas kernels, tables(): pl.pallas_call(functools.partial(table_kernel, group, terms, sources, tap...  3.98 us
    pallas_call x2, Pallas kernels, merge(): pl.pallas_call(functools.partial(merge_kernel, group, segments, chunk, fi...  3.72 us
    ppermute x4, waiting for transfers between devices, on_device(): mine.append(lax.ppermute(early_pack, ('sub', 'rng'), route))  2.73 us
    pallas_call x2, Pallas kernels, form(): pl.pallas_call(functools.partial(form_kernel, group, pulse_count, len(blo...  2.22 us
  transfers between devices with their start and end apart: 20, of which 5 were waited for; matrix products, arithmetic and copies ran while one was open for 0% of the time, Pallas kernels for 24%

profile of v1, /device:TPU:0, one launch (start us, length us, event | category | flops | bytes accessed | tf_op | source)
XLA Modules:
  0.0 59.4 jit_solution(13075592373815375553)
XLA Ops:
  0.0 1.4 %cut.1 = (bf16[2,128,512]{2,1,0:T(8,128)(2,1)S(1)}, bf16[2,128,512]{2,1,0:T(8,128)(2,1)S(1)}, bf16[2,128,512]{2,1,0:T(8,128)(2,1)S(1)}, bf16[2,128,512]{2,1,0:T(...) custom-call(bf16[2,4,128,512]{3,2,1,0:T(8,128)(2,1)} %echoes.1, s32[1,3,2,256]{3,2,1,0:T(2,128)} %offset.1, ...), custom_call_target="tpu_custom_call" | custom-call | flops 1000000000 | bytes 1048576 | tf_op jit(solution)/shard_map/cut/pallas_call | solution.py:435
  1.5 4.0 %collective-permute-start.6 = (bf16[56,256]{1,0:T(8,128)(2,1)S(1)}, bf16[56,256]{1,0:T(8,128)(2,1)S(1)}, u32[]{:S(2)}, u32[]{:S(2)}) collective-permute-start(bf16[56,256]{1,0:T(8,128)(2,1)S(1)} %get-tuple-element.35.refs_0_), channel_id=1, source_target_pairs={{0,12},{1,9},{2,14},{3,11},{4,8},{5,13},{6,10},{7,15},{8,4},{9,1},... | collective-permute-start | bytes 86024 | tf_op jit(solution)/shard_map/ppermute | solution.py:460
  5.5 2.4 %collective-permute-start.4 = (bf16[56,256]{1,0:T(8,128)(2,1)S(1)}, bf16[56,256]{1,0:T(8,128)(2,1)S(1)}, u32[]{:S(2)}, u32[]{:S(2)}) collective-permute-start(bf16[56,256]{1,0:T(8,128)(2,1)S(1)} %get-tuple-element.35.refs_0_), channel_id=1, source_target_pairs={{0,28},{1,25},{2,30},{3,27},{4,24},{5,29},{6,26},{7,31},{8,20},{9,... | collective-permute-start | bytes 86024 | tf_op jit(solution)/shard_map/ppermute | solution.py:460
  8.3 1.2 %collective-permute-start.7 = (bf16[56,256]{1,0:T(8,128)(2,1)S(1)}, bf16[56,256]{1,0:T(8,128)(2,1)S(1)}, u32[]{:S(2)}, u32[]{:S(2)}) collective-permute-start(bf16[56,256]{1,0:T(8,128)(2,1)S(1)} %get-tuple-element.35.refs_0_), channel_id=1, source_target_pairs={{0,4},{1,5},{2,6},{3,7},{4,0},{5,1},{6,2},{7,3},{8,12},{9,13},{10,... | collective-permute-start | bytes 86024 | tf_op jit(solution)/shard_map/ppermute | solution.py:460
  9.6 1.6 %collective-permute-start.10 = (bf16[56,256]{1,0:T(8,128)(2,1)S(1)}, bf16[56,256]{1,0:T(8,128)(2,1)S(1)}, u32[]{:S(2)}, u32[]{:S(2)}) collective-permute-start(bf16[56,256]{1,0:T(8,128)(2,1)S(1)} %collective-permute-done.6.refs_3_), channel_id=1, source_target_pairs={{0,1},{1,0},{2,3},{3,2},{4,5},{5,4},{6,7},{7,6},{8,9},{9,8},{10,11... | collective-permute-start | bytes 86024 | tf_op jit(solution)/shard_map/ppermute | solution.py:21
  12.1 1.8 %collective-permute-done.5.refs_2_ = bf16[56,256]{1,0:T(8,128)(2,1)S(1)} collective-permute-done((bf16[56,256]{1,0:T(8,128)(2,1)S(1)}, bf16[56,256]{1,0:T(8,128)(2,1)S(1)}, u32[]{:S(2)}, u32[]{:S(2)}) %collective-permute-start.5) | collective-permute-done | bytes 28704 | tf_op jit(solution)/shard_map/ppermute | solution.py:460
  14.4 1.5 %collective-permute-start.1 = (bf16[2,128,512]{2,1,0:T(8,128)(2,1)S(1)}, bf16[2,128,512]{2,1,0:T(8,128)(2,1)S(1)}, u32[]{:S(2)}, u32[]{:S(2)}) collective-permute-start(bf16[2,128,512]{2,1,0:T(8,128)(2,1)S(1)} %get-tuple-element.33), channel_id=1, source_target_pairs={{0,2},{1,3},{2,0},{3,1},{4,6},{5,7},{6,4},{7,5},{8,10},{9,11},{10,... | collective-permute-start | bytes 786440 | tf_op jit(solution)/shard_map/ppermute | solution.py:21
  16.0 2.7 %shard_map.74 = (bf16[8,4,256,256]{3,2,1,0:T(8,128)(2,1)S(1)}, f32[8,4,2,136,256]{4,3,2,1,0:T(8,128)S(1)}) custom-call(bf16[56,256]{1,0:T(8,128)(2,1)S(1)} %get-tuple-element.35.refs_0_, bf16[56,256]{1,0:T(8,128)(2,1)S(1)} %collective-permute-done.4.refs_1_, bf16[56,256]{1,0:T(8,128)(2,1)S(1)} %collective-permute-done.5.refs_2_, ...), custom_call_target="tpu_custom_call" | custom-call | flops 2000000000 | bytes 1048576 | tf_op jit(solution)/shard_map/pallas_call | solution.py:492
  18.7 5.1 %collective-permute-done.1.refs_2_ = bf16[2,128,512]{2,1,0:T(8,128)(2,1)S(1)} collective-permute-done((bf16[2,128,512]{2,1,0:T(8,128)(2,1)S(1)}, bf16[2,128,512]{2,1,0:T(8,128)(2,1)S(1)}, u32[]{:S(2)}, u32[]{:S(2)}) %collective-permute-start.1) | collective-permute-done | bytes 262176 | tf_op jit(solution)/shard_map/ppermute | solution.py:21
  23.8 1.3 %collective-permute-start.3 = (bf16[4,2,8,512]{3,2,1,0:T(8,128)(2,1)S(1)}, bf16[4,2,8,512]{3,2,1,0:T(8,128)(2,1)S(1)}, u32[]{:S(2)}, u32[]{:S(2)}) collective-permute-start(bf16[4,2,8,512]{3,2,1,0:T(8,128)(2,1)S(1)} %pad_maximum_fusion), channel_id=1, source_target_pairs={{1,28},{2,29},{3,30},{4,0},{5,1},{6,2},{7,3},{8,4},{9,5},{10,6},{1... | collective-permute-start | bytes 196616 | tf_op jit(solution)/shard_map/ppermute | solution.py:489
  25.1 1.2 %shard_map.75.refs_0_ = f32[8,2,2,96,128]{4,3,2,1,0:T(8,128)S(1)} custom-call(s32[8]{0:T(128)S(1)} %copy-done.1, bf16[2,128,512]{2,1,0:T(8,128)(2,1)S(1)} %get-tuple-element.31.refs_0_, bf16[2,128,512]{2,1,0:T(8,128)(2,1)S(1)} %collective-permute-done.refs_1_, bf16[2,128,512]{2,1,0:T(8,128)(2,1)S(1)} %collective-permute-done.1.refs_2_, ...), custom_call_target="tpu_custom_call" | custom-call | flops 1000000000 | bytes 1048576 | tf_op jit(solution)/shard_map/pallas_call | solution.py:530
  26.3 1.6 %shard_map.76 = (bf16[328,128]{1,0:T(8,128)(2,1)S(1)}, bf16[328,128]{1,0:T(8,128)(2,1)S(1)}, bf16[328,128]{1,0:T(8,128)(2,1)S(1)}, bf16[328,128]{1,0:T(8,128)(2,...) custom-call(f32[8,2,2,96,128]{4,3,2,1,0:T(8,128)S(1)} %shard_map.75., ...), custom_call_target="tpu_custom_call" | custom-call | flops 4000000000 | bytes 1048576 | tf_op jit(solution)/shard_map/pallas_call | solution.py:542
  27.9 5.1 %collective-permute-start.18 = (bf16[328,128]{1,0:T(8,128)(2,1)S(1)}, bf16[328,128]{1,0:T(8,128)(2,1)S(1)}, u32[]{:S(2)}, u32[]{:S(2)}) collective-permute-start(bf16[328,128]{1,0:T(8,128)(2,1)S(1)} %get-tuple-element.55), channel_id=1, source_target_pairs={{0,28},{4,24},{8,20},{12,16},{16,12},{20,8},{24,4},{28,0},{1,29},{... | collective-permute-start | bytes 251912 | tf_op jit(solution)/shard_map/ppermute | solution.py:21
  33.9 1.0 %shard_map.73.refs_1_ = f32[8,2,2,48,128]{4,3,2,1,0:T(8,128)S(1)} custom-call(s32[8]{0:T(128)S(1)} %copy-done.1, bf16[2,128,512]{2,1,0:T(8,128)(2,1)S(1)} %get-tuple-element.31.refs_0_, bf16[2,128,512]{2,1,0:T(8,128)(2,1)S(1)} %collective-permute-done.refs_1_, bf16[2,128,512]{2,1,0:T(8,128)(2,1)S(1)} %collective-permute-done.1.refs_2_, ...), custom_call_target="tpu_custom_call" | custom-call | flops 1000000000 | bytes 1048576 | tf_op jit(solution)/shard_map/pallas_call | solution.py:530
  34.9 2.2 %shard_map.77 = (bf16[528,128]{1,0:T(8,128)(2,1)S(1)}, bf16[528,128]{1,0:T(8,128)(2,1)S(1)}, bf16[528,128]{1,0:T(8,128)(2,1)S(1)}, bf16[528,128]{1,0:T(8,128)(2,...) custom-call(s32[8]{0:T(128)S(1)} %copy-done.1, ...), custom_call_target="tpu_custom_call" | custom-call | flops 4000000000 | bytes 1048576 | tf_op jit(solution)/shard_map/pallas_call | solution.py:542
  37.1 1.9 %collective-permute-start.14 = (bf16[528,128]{1,0:T(8,128)(2,1)S(1)}, bf16[528,128]{1,0:T(8,128)(2,1)S(1)}, u32[]{:S(2)}, u32[]{:S(2)}) collective-permute-start(bf16[528,128]{1,0:T(8,128)(2,1)S(1)} %get-tuple-element.50), channel_id=1, source_target_pairs={{0,20},{4,16},{8,28},{12,24},{16,4},{20,0},{24,12},{28,8},{1,21},{... | collective-permute-start | bytes 405512 | tf_op jit(solution)/shard_map/ppermute | solution.py:21
  39.0 2.6 %collective-permute-start.15 = (bf16[528,128]{1,0:T(8,128)(2,1)S(1)}, bf16[528,128]{1,0:T(8,128)(2,1)S(1)}, u32[]{:S(2)}, u32[]{:S(2)}) collective-permute-start(bf16[528,128]{1,0:T(8,128)(2,1)S(1)} %get-tuple-element.51), channel_id=1, source_target_pairs={{0,12},{4,8},{8,4},{12,0},{16,28},{20,24},{24,20},{28,16},{1,13},{... | collective-permute-start | bytes 405512 | tf_op jit(solution)/shard_map/ppermute | solution.py:21
  42.3 1.5 %collective-permute-start.17 = (bf16[528,128]{1,0:T(8,128)(2,1)S(1)}, bf16[528,128]{1,0:T(8,128)(2,1)S(1)}, u32[]{:S(2)}, u32[]{:S(2)}) collective-permute-start(bf16[528,128]{1,0:T(8,128)(2,1)S(1)} %get-tuple-element.53), channel_id=1, source_target_pairs={{0,4},{4,0},{8,12},{12,8},{16,20},{20,16},{24,28},{28,24},{1,5},{5... | collective-permute-start | bytes 405512 | tf_op jit(solution)/shard_map/ppermute | solution.py:21
  43.8 1.3 %shard_map.78 = (bf16[1,2,256,256]{3,2,1,0:T(8,128)(2,1)S(1)}, f32[8,2,2,128,256]{4,3,2,1,0:T(8,128)S(1)}) custom-call(bf16[32,256]{1,0:T(8,128)(2,1)S(1)} %get-tuple-element.45.refs_0_), custom_call_target="tpu_custom_call" | custom-call | flops 2000000000 | bytes 1048576 | tf_op jit(solution)/shard_map/pallas_call | solution.py:492
  45.7 1.1 %final.5.refs_6_ = bf16[2,1024,256]{2,1,0:T(8,128)(2,1)} custom-call(bf16[528,128]{1,0:T(8,128)(2,1)S(1)} %get-tuple-element.54.refs_0_, bf16[328,128]{1,0:T(8,128)(2,1)S(1)} %collective-permute-done.18.refs_1_, bf16[328,128]{1,0:T(8,128)(2,1)S(1)} %collective-permute-done.19.refs_2_, bf16[1,2,256,256]{3,2,1,0:T(8,128)(2,1)S(1)} %get-tuple-element.46.refs_3_.refs_4_.refs_1_, ...), custom_call_target="tpu_custom_call" | custom-call | flops 1000000000 | bytes 1048576 | tf_op jit(solution)/shard_map/final/pallas_call | solution.py:592
  46.9 3.3 %collective-permute-start.12 = (bf16[200,128]{1,0:T(8,128)(2,1)S(1)}, bf16[200,128]{1,0:T(8,128)(2,1)S(1)}, u32[]{:S(2)}, u32[]{:S(2)}) collective-permute-start(bf16[200,128]{1,0:T(8,128)(2,1)S(1)} %get-tuple-element.48), channel_id=1, source_target_pairs={{0,28},{4,24},{8,20},{12,16},{16,12},{20,8},{24,4},{28,0},{1,29},{... | collective-permute-start | bytes 153608 | tf_op jit(solution)/shard_map/ppermute | solution.py:21
  50.2 1.2 %collective-permute-start.11 = (bf16[200,128]{1,0:T(8,128)(2,1)S(1)}, bf16[200,128]{1,0:T(8,128)(2,1)S(1)}, u32[]{:S(2)}, u32[]{:S(2)}) collective-permute-start(bf16[200,128]{1,0:T(8,128)(2,1)S(1)} %get-tuple-element.44), channel_id=1, source_target_pairs={{0,24},{4,28},{8,16},{12,20},{16,8},{20,12},{24,0},{28,4},{1,25},{... | collective-permute-start | bytes 153608 | tf_op jit(solution)/shard_map/ppermute | solution.py:21
  51.4 4.2 %collective-permute-done.16.refs_2_ = bf16[528,128]{1,0:T(8,128)(2,1)S(1)} collective-permute-done((bf16[528,128]{1,0:T(8,128)(2,1)S(1)}, bf16[528,128]{1,0:T(8,128)(2,1)S(1)}, u32[]{:S(2)}, u32[]{:S(2)}) %collective-permute-start.16) | collective-permute-done | bytes 135200 | tf_op jit(solution)/shard_map/ppermute | solution.py:21
  55.5 1.3 %final.6.refs_3_ = bf16[2,1024,256]{2,1,0:T(8,128)(2,1)} custom-call(bf16[528,128]{1,0:T(8,128)(2,1)S(1)} %collective-permute-done.14.refs_0_, bf16[528,128]{1,0:T(8,128)(2,1)S(1)} %collective-permute-done.15.refs_1_, bf16[528,128]{1,0:T(8,128)(2,1)S(1)} %collective-permute-done.16.refs_2_, ...), custom_call_target="tpu_custom_call", output_to_operand_aliasing={{}: (6, {})} | custom-call | flops 1000000000 | bytes 1048576 | tf_op jit(solution)/shard_map/final/pallas_call | solution.py:592
  (37 shorter events, 6.8 us)
Async XLA Ops:
  1.4 23.7 %copy-start = (bf16[2,256,256]{2,1,0:T(8,128)(2,1)S(1)}, bf16[2,256,256]{2,1,0:T(8,128)(2,1)}, u32[]{:S(2)}) copy-start(bf16[2,256,256]{2,1,0:T(8,128)(2,1)} %refs_3_.1) | copy-start | bytes 786436
  1.4 23.7 %copy-start.1 = (s32[8]{0:T(128)S(1)}, s32[8]{0:T(128)}, u32[]{:S(2)}) copy-start(s32[8]{0:T(128)} %refs_0_.1) | copy-start | bytes 100
  1.5 8.1 %collective-permute-start.6 = (bf16[56,256]{1,0:T(8,128)(2,1)S(1)}, bf16[56,256]{1,0:T(8,128)(2,1)S(1)}, u32[]{:S(2)}, u32[]{:S(2)}) collective-permute-start(bf16[56,256]{1,0:T(8,128)(2,1)S(1)} %get-tuple-element.35.refs_0_), channel_id=1, source_target_pairs={{0,12},{1,9},{2,14},{3,11},{4,8},{5,13},{6,10},{7,15},{8,4},{9,1},... | collective-permute-start | bytes 86024 | tf_op jit(solution)/shard_map/ppermute | solution.py:460
  5.5 6.6 %collective-permute-start.4 = (bf16[56,256]{1,0:T(8,128)(2,1)S(1)}, bf16[56,256]{1,0:T(8,128)(2,1)S(1)}, u32[]{:S(2)}, u32[]{:S(2)}) collective-permute-start(bf16[56,256]{1,0:T(8,128)(2,1)S(1)} %get-tuple-element.35.refs_0_), channel_id=1, source_target_pairs={{0,28},{1,25},{2,30},{3,27},{4,24},{5,29},{6,26},{7,31},{8,20},{9,... | collective-permute-start | bytes 86024 | tf_op jit(solution)/shard_map/ppermute | solution.py:460
  7.9 6.0 %collective-permute-start.5 = (bf16[56,256]{1,0:T(8,128)(2,1)S(1)}, bf16[56,256]{1,0:T(8,128)(2,1)S(1)}, u32[]{:S(2)}, u32[]{:S(2)}) collective-permute-start(bf16[56,256]{1,0:T(8,128)(2,1)S(1)} %get-tuple-element.35.refs_0_), channel_id=1, source_target_pairs={{0,20},{1,17},{2,22},{3,19},{4,16},{5,21},{6,18},{7,23},{8,28},{9,... | collective-permute-start | bytes 86024 | tf_op jit(solution)/shard_map/ppermute | solution.py:460
  8.3 5.6 %collective-permute-start.7 = (bf16[56,256]{1,0:T(8,128)(2,1)S(1)}, bf16[56,256]{1,0:T(8,128)(2,1)S(1)}, u32[]{:S(2)}, u32[]{:S(2)}) collective-permute-start(bf16[56,256]{1,0:T(8,128)(2,1)S(1)} %get-tuple-element.35.refs_0_), channel_id=1, source_target_pairs={{0,4},{1,5},{2,6},{3,7},{4,0},{5,1},{6,2},{7,3},{8,12},{9,13},{10,... | collective-permute-start | bytes 86024 | tf_op jit(solution)/shard_map/ppermute | solution.py:460
  9.6 9.1 %collective-permute-start.2 = (bf16[2,128,512]{2,1,0:T(8,128)(2,1)S(1)}, bf16[2,128,512]{2,1,0:T(8,128)(2,1)S(1)}, u32[]{:S(2)}, u32[]{:S(2)}) collective-permute-start(bf16[2,128,512]{2,1,0:T(8,128)(2,1)S(1)} %get-tuple-element.34), channel_id=1, source_target_pairs={{0,3},{1,2},{2,1},{3,0},{4,7},{5,6},{6,5},{7,4},{8,11},{9,10},{10,... | collective-permute-start | bytes 786440 | tf_op jit(solution)/shard_map/ppermute | solution.py:21
  9.6 4.9 %collective-permute-start.10 = (bf16[56,256]{1,0:T(8,128)(2,1)S(1)}, bf16[56,256]{1,0:T(8,128)(2,1)S(1)}, u32[]{:S(2)}, u32[]{:S(2)}) collective-permute-start(bf16[56,256]{1,0:T(8,128)(2,1)S(1)} %collective-permute-done.6.refs_3_), channel_id=1, source_target_pairs={{0,1},{1,0},{2,3},{3,2},{4,5},{5,4},{6,7},{7,6},{8,9},{9,8},{10,11... | collective-permute-start | bytes 86024 | tf_op jit(solution)/shard_map/ppermute | solution.py:21
  12.1 3.9 %collective-permute-start.8 = (bf16[56,256]{1,0:T(8,128)(2,1)S(1)}, bf16[56,256]{1,0:T(8,128)(2,1)S(1)}, u32[]{:S(2)}, u32[]{:S(2)}) collective-permute-start(bf16[56,256]{1,0:T(8,128)(2,1)S(1)} %collective-permute-done.4.refs_1_), channel_id=1, source_target_pairs={{0,1},{1,0},{2,3},{3,2},{4,5},{5,4},{6,7},{7,6},{8,9},{9,8},{10,11... | collective-permute-start | bytes 86024 | tf_op jit(solution)/shard_map/ppermute | solution.py:21
  13.9 2.0 %collective-permute-start.9 = (bf16[56,256]{1,0:T(8,128)(2,1)S(1)}, bf16[56,256]{1,0:T(8,128)(2,1)S(1)}, u32[]{:S(2)}, u32[]{:S(2)}) collective-permute-start(bf16[56,256]{1,0:T(8,128)(2,1)S(1)} %collective-permute-done.5.refs_2_), channel_id=1, source_target_pairs={{0,1},{1,0},{2,3},{3,2},{4,5},{5,4},{6,7},{7,6},{8,9},{9,8},{10,11... | collective-permute-start | bytes 86024 | tf_op jit(solution)/shard_map/ppermute | solution.py:21
  13.9 9.9 %collective-permute-start = (bf16[2,128,512]{2,1,0:T(8,128)(2,1)S(1)}, bf16[2,128,512]{2,1,0:T(8,128)(2,1)S(1)}, u32[]{:S(2)}, u32[]{:S(2)}) collective-permute-start(bf16[2,128,512]{2,1,0:T(8,128)(2,1)S(1)} %get-tuple-element.32), channel_id=1, source_target_pairs={{0,1},{1,0},{2,3},{3,2},{4,5},{5,4},{6,7},{7,6},{8,9},{9,8},{10,11... | collective-permute-start | bytes 786440 | tf_op jit(solution)/shard_map/ppermute | solution.py:21
  14.4 9.3 %collective-permute-start.1 = (bf16[2,128,512]{2,1,0:T(8,128)(2,1)S(1)}, bf16[2,128,512]{2,1,0:T(8,128)(2,1)S(1)}, u32[]{:S(2)}, u32[]{:S(2)}) collective-permute-start(bf16[2,128,512]{2,1,0:T(8,128)(2,1)S(1)} %get-tuple-element.33), channel_id=1, source_target_pairs={{0,2},{1,3},{2,0},{3,1},{4,6},{5,7},{6,4},{7,5},{8,10},{9,11},{10,... | collective-permute-start | bytes 786440 | tf_op jit(solution)/shard_map/ppermute | solution.py:21
  23.8 11.1 %collective-permute-start.3 = (bf16[4,2,8,512]{3,2,1,0:T(8,128)(2,1)S(1)}, bf16[4,2,8,512]{3,2,1,0:T(8,128)(2,1)S(1)}, u32[]{:S(2)}, u32[]{:S(2)}) collective-permute-start(bf16[4,2,8,512]{3,2,1,0:T(8,128)(2,1)S(1)} %pad_maximum_fusion), channel_id=1, source_target_pairs={{1,28},{2,29},{3,30},{4,0},{5,1},{6,2},{7,3},{8,4},{9,5},{10,6},{1... | collective-permute-start | bytes 196616 | tf_op jit(solution)/shard_map/ppermute | solution.py:489
  27.9 14.4 %collective-permute-start.18 = (bf16[328,128]{1,0:T(8,128)(2,1)S(1)}, bf16[328,128]{1,0:T(8,128)(2,1)S(1)}, u32[]{:S(2)}, u32[]{:S(2)}) collective-permute-start(bf16[328,128]{1,0:T(8,128)(2,1)S(1)} %get-tuple-element.55), channel_id=1, source_target_pairs={{0,28},{4,24},{8,20},{12,16},{16,12},{20,8},{24,4},{28,0},{1,29},{... | collective-permute-start | bytes 251912 | tf_op jit(solution)/shard_map/ppermute | solution.py:21
  33.0 12.1 %collective-permute-start.19 = (bf16[328,128]{1,0:T(8,128)(2,1)S(1)}, bf16[328,128]{1,0:T(8,128)(2,1)S(1)}, u32[]{:S(2)}, u32[]{:S(2)}) collective-permute-start(bf16[328,128]{1,0:T(8,128)(2,1)S(1)} %get-tuple-element.56), channel_id=1, source_target_pairs={{0,24},{4,28},{8,16},{12,20},{16,8},{20,12},{24,0},{28,4},{1,25},{... | collective-permute-start | bytes 251912 | tf_op jit(solution)/shard_map/ppermute | solution.py:21
  37.1 9.8 %collective-permute-start.14 = (bf16[528,128]{1,0:T(8,128)(2,1)S(1)}, bf16[528,128]{1,0:T(8,128)(2,1)S(1)}, u32[]{:S(2)}, u32[]{:S(2)}) collective-permute-start(bf16[528,128]{1,0:T(8,128)(2,1)S(1)} %get-tuple-element.50), channel_id=1, source_target_pairs={{0,20},{4,16},{8,28},{12,24},{16,4},{20,0},{24,12},{28,8},{1,21},{... | collective-permute-start | bytes 405512 | tf_op jit(solution)/shard_map/ppermute | solution.py:21
  39.0 11.2 %collective-permute-start.15 = (bf16[528,128]{1,0:T(8,128)(2,1)S(1)}, bf16[528,128]{1,0:T(8,128)(2,1)S(1)}, u32[]{:S(2)}, u32[]{:S(2)}) collective-permute-start(bf16[528,128]{1,0:T(8,128)(2,1)S(1)} %get-tuple-element.51), channel_id=1, source_target_pairs={{0,12},{4,8},{8,4},{12,0},{16,28},{20,24},{24,20},{28,16},{1,13},{... | collective-permute-start | bytes 405512 | tf_op jit(solution)/shard_map/ppermute | solution.py:21
  41.5 14.0 %collective-permute-start.16 = (bf16[528,128]{1,0:T(8,128)(2,1)S(1)}, bf16[528,128]{1,0:T(8,128)(2,1)S(1)}, u32[]{:S(2)}, u32[]{:S(2)}) collective-permute-start(bf16[528,128]{1,0:T(8,128)(2,1)S(1)} %get-tuple-element.52), channel_id=1, source_target_pairs={{0,8},{4,12},{8,0},{12,4},{16,24},{20,28},{24,16},{28,20},{1,9},{5... | collective-permute-start | bytes 405512 | tf_op jit(solution)/shard_map/ppermute | solution.py:21
  42.3 13.2 %collective-permute-start.17 = (bf16[528,128]{1,0:T(8,128)(2,1)S(1)}, bf16[528,128]{1,0:T(8,128)(2,1)S(1)}, u32[]{:S(2)}, u32[]{:S(2)}) collective-permute-start(bf16[528,128]{1,0:T(8,128)(2,1)S(1)} %get-tuple-element.53), channel_id=1, source_target_pairs={{0,4},{4,0},{8,12},{12,8},{16,20},{20,16},{24,28},{28,24},{1,5},{5... | collective-permute-start | bytes 405512 | tf_op jit(solution)/shard_map/ppermute | solution.py:21
  45.1 11.7 %collective-permute-start.13 = (bf16[528,128]{1,0:T(8,128)(2,1)S(1)}, bf16[528,128]{1,0:T(8,128)(2,1)S(1)}, u32[]{:S(2)}, u32[]{:S(2)}) collective-permute-start(bf16[528,128]{1,0:T(8,128)(2,1)S(1)} %get-tuple-element.49), channel_id=1, source_target_pairs={{0,16},{4,20},{8,24},{12,28},{16,0},{20,4},{24,8},{28,12},{1,17},{... | collective-permute-start | bytes 405512 | tf_op jit(solution)/shard_map/ppermute | solution.py:21
  46.9 10.9 %collective-permute-start.12 = (bf16[200,128]{1,0:T(8,128)(2,1)S(1)}, bf16[200,128]{1,0:T(8,128)(2,1)S(1)}, u32[]{:S(2)}, u32[]{:S(2)}) collective-permute-start(bf16[200,128]{1,0:T(8,128)(2,1)S(1)} %get-tuple-element.48), channel_id=1, source_target_pairs={{0,28},{4,24},{8,20},{12,16},{16,12},{20,8},{24,4},{28,0},{1,29},{... | collective-permute-start | bytes 153608 | tf_op jit(solution)/shard_map/ppermute | solution.py:21
  50.2 8.4 %collective-permute-start.11 = (bf16[200,128]{1,0:T(8,128)(2,1)S(1)}, bf16[200,128]{1,0:T(8,128)(2,1)S(1)}, u32[]{:S(2)}, u32[]{:S(2)}) collective-permute-start(bf16[200,128]{1,0:T(8,128)(2,1)S(1)} %get-tuple-element.44), channel_id=1, source_target_pairs={{0,24},{4,28},{8,16},{12,20},{16,8},{20,12},{24,0},{28,4},{1,25},{... | collective-permute-start | bytes 153608 | tf_op jit(solution)/shard_map/ppermute | solution.py:21

commit v2 on v1

--- a/solution.py
+++ b/solution.py
@@ -580,7 +580,10 @@
 
     last_bands, last_waves = tables(late, None, 1, rows, [late_pack])
     result = None
-    turns = [[(0, None)] + upper_order, lower_order[:-3]] + [[key] for key in lower_order[-3:]]
+    middle, slow = lower_order[:1], lower_order[-3:]
+    for key in lower_order[1:-3]:
+        (slow if key[0] == 2 else middle).append(key)
+    turns = [[(0, None)] + upper_order, middle, slow]
     for chosen in turns:
         count = len(chosen)
         jobs = []

time: 59.6 us -> 59.9 us (level)
  Pallas kernels: 16.3 us -> 14.8 us
  starting transfers between devices: 30.8 us -> 32 us
  waiting for transfers between devices: 12.1 us -> 12.7 us
    pallas_call x5 -> x3, Pallas kernels: 4.93 us -> 3.41 us  [on_device(): pl.pallas_call(functools.partial(final_kernel, jobs, count, group, rows,...]
    ppermute x15, starting transfers between devices: 21.4 us -> 22.6 us  [exchanged(): lax.ppermute(block, axis, [(source, source ^ mask) for source in range(co...]
  transfers between devices with their start and end apart: 20 -> 20, of which waited for: 5 -> 6; matrix products, arithmetic and copies ran while one was open for 0% -> 0% of each run, Pallas kernels for 24% -> 20%
where the time goes in v2:
time: 59.9 us; the launch traced here: 59.7 us
  starting transfers between devices  32 us (53%)
  Pallas kernels  14.8 us (25%)
  waiting for transfers between devices  12.7 us (21%)
    ppermute x15, starting transfers between devices, exchanged(): lax.ppermute(block, axis, [(source, source ^ mask) for source in range(co...  22.6 us
    ppermute x15, waiting for transfers between devices, exchanged(): lax.ppermute(block, axis, [(source, source ^ mask) for source in range(co...  9.96 us
    ppermute x4, starting transfers between devices, on_device(): mine.append(lax.ppermute(early_pack, ('sub', 'rng'), route))  8.1 us
    pallas_call x2, Pallas kernels, tables(): pl.pallas_call(functools.partial(table_kernel, group, terms, sources, tap...  3.98 us
    pallas_call x2, Pallas kernels, merge(): pl.pallas_call(functools.partial(merge_kernel, group, segments, chunk, fi...  3.72 us
    pallas_call x3, Pallas kernels, on_device(): pl.pallas_call(functools.partial(final_kernel, jobs, count, group, rows,...  3.41 us
    ppermute x4, waiting for transfers between devices, on_device(): mine.append(lax.ppermute(early_pack, ('sub', 'rng'), route))  2.73 us
    pallas_call x2, Pallas kernels, form(): pl.pallas_call(functools.partial(form_kernel, group, pulse_count, len(blo...  2.22 us
  transfers between devices with their start and end apart: 20, of which 6 were waited for; matrix products, arithmetic and copies ran while one was open for 0% of the time, Pallas kernels for 20%

profile of v2, /device:TPU:0, one launch (start us, length us, event | category | flops | bytes accessed | tf_op | source)
XLA Modules:
  0.0 59.7 jit_solution(18220191545068875466)
XLA Ops:
  0.0 1.4 %cut.1 = (bf16[2,128,512]{2,1,0:T(8,128)(2,1)S(1)}, bf16[2,128,512]{2,1,0:T(8,128)(2,1)S(1)}, bf16[2,128,512]{2,1,0:T(8,128)(2,1)S(1)}, bf16[2,128,512]{2,1,0:T(...) custom-call(bf16[2,4,128,512]{3,2,1,0:T(8,128)(2,1)} %echoes.1, s32[1,3,2,256]{3,2,1,0:T(2,128)} %offset.1, ...), custom_call_target="tpu_custom_call" | custom-call | flops 1000000000 | bytes 1048576 | tf_op jit(solution)/shard_map/cut/pallas_call | solution.py:435
  1.5 4.0 %collective-permute-start.6 = (bf16[56,256]{1,0:T(8,128)(2,1)S(1)}, bf16[56,256]{1,0:T(8,128)(2,1)S(1)}, u32[]{:S(2)}, u32[]{:S(2)}) collective-permute-start(bf16[56,256]{1,0:T(8,128)(2,1)S(1)} %get-tuple-element.35.refs_0_), channel_id=1, source_target_pairs={{0,12},{1,9},{2,14},{3,11},{4,8},{5,13},{6,10},{7,15},{8,4},{9,1},... | collective-permute-start | bytes 86024 | tf_op jit(solution)/shard_map/ppermute | solution.py:460
  5.5 2.4 %collective-permute-start.4 = (bf16[56,256]{1,0:T(8,128)(2,1)S(1)}, bf16[56,256]{1,0:T(8,128)(2,1)S(1)}, u32[]{:S(2)}, u32[]{:S(2)}) collective-permute-start(bf16[56,256]{1,0:T(8,128)(2,1)S(1)} %get-tuple-element.35.refs_0_), channel_id=1, source_target_pairs={{0,28},{1,25},{2,30},{3,27},{4,24},{5,29},{6,26},{7,31},{8,20},{9,... | collective-permute-start | bytes 86024 | tf_op jit(solution)/shard_map/ppermute | solution.py:460
  8.3 1.2 %collective-permute-start.7 = (bf16[56,256]{1,0:T(8,128)(2,1)S(1)}, bf16[56,256]{1,0:T(8,128)(2,1)S(1)}, u32[]{:S(2)}, u32[]{:S(2)}) collective-permute-start(bf16[56,256]{1,0:T(8,128)(2,1)S(1)} %get-tuple-element.35.refs_0_), channel_id=1, source_target_pairs={{0,4},{1,5},{2,6},{3,7},{4,0},{5,1},{6,2},{7,3},{8,12},{9,13},{10,... | collective-permute-start | bytes 86024 | tf_op jit(solution)/shard_map/ppermute | solution.py:460
  9.6 1.6 %collective-permute-start.10 = (bf16[56,256]{1,0:T(8,128)(2,1)S(1)}, bf16[56,256]{1,0:T(8,128)(2,1)S(1)}, u32[]{:S(2)}, u32[]{:S(2)}) collective-permute-start(bf16[56,256]{1,0:T(8,128)(2,1)S(1)} %collective-permute-done.6.refs_3_), channel_id=1, source_target_pairs={{0,1},{1,0},{2,3},{3,2},{4,5},{5,4},{6,7},{7,6},{8,9},{9,8},{10,11... | collective-permute-start | bytes 86024 | tf_op jit(solution)/shard_map/ppermute | solution.py:21
  12.1 1.8 %collective-permute-done.5.refs_2_ = bf16[56,256]{1,0:T(8,128)(2,1)S(1)} collective-permute-done((bf16[56,256]{1,0:T(8,128)(2,1)S(1)}, bf16[56,256]{1,0:T(8,128)(2,1)S(1)}, u32[]{:S(2)}, u32[]{:S(2)}) %collective-permute-start.5) | collective-permute-done | bytes 28704 | tf_op jit(solution)/shard_map/ppermute | solution.py:460
  14.4 1.5 %collective-permute-start.1 = (bf16[2,128,512]{2,1,0:T(8,128)(2,1)S(1)}, bf16[2,128,512]{2,1,0:T(8,128)(2,1)S(1)}, u32[]{:S(2)}, u32[]{:S(2)}) collective-permute-start(bf16[2,128,512]{2,1,0:T(8,128)(2,1)S(1)} %get-tuple-element.33), channel_id=1, source_target_pairs={{0,2},{1,3},{2,0},{3,1},{4,6},{5,7},{6,4},{7,5},{8,10},{9,11},{10,... | collective-permute-start | bytes 786440 | tf_op jit(solution)/shard_map/ppermute | solution.py:21
  16.0 2.7 %shard_map.74 = (bf16[8,4,256,256]{3,2,1,0:T(8,128)(2,1)S(1)}, f32[8,4,2,136,256]{4,3,2,1,0:T(8,128)S(1)}) custom-call(bf16[56,256]{1,0:T(8,128)(2,1)S(1)} %get-tuple-element.35.refs_0_, bf16[56,256]{1,0:T(8,128)(2,1)S(1)} %collective-permute-done.4.refs_1_, bf16[56,256]{1,0:T(8,128)(2,1)S(1)} %collective-permute-done.5.refs_2_, ...), custom_call_target="tpu_custom_call" | custom-call | flops 2000000000 | bytes 1048576 | tf_op jit(solution)/shard_map/pallas_call | solution.py:492
  18.7 5.1 %collective-permute-done.1.refs_2_ = bf16[2,128,512]{2,1,0:T(8,128)(2,1)S(1)} collective-permute-done((bf16[2,128,512]{2,1,0:T(8,128)(2,1)S(1)}, bf16[2,128,512]{2,1,0:T(8,128)(2,1)S(1)}, u32[]{:S(2)}, u32[]{:S(2)}) %collective-permute-start.1) | collective-permute-done | bytes 262176 | tf_op jit(solution)/shard_map/ppermute | solution.py:21
  23.8 1.3 %collective-permute-start.3 = (bf16[4,2,8,512]{3,2,1,0:T(8,128)(2,1)S(1)}, bf16[4,2,8,512]{3,2,1,0:T(8,128)(2,1)S(1)}, u32[]{:S(2)}, u32[]{:S(2)}) collective-permute-start(bf16[4,2,8,512]{3,2,1,0:T(8,128)(2,1)S(1)} %pad_maximum_fusion), channel_id=1, source_target_pairs={{1,28},{2,29},{3,30},{4,0},{5,1},{6,2},{7,3},{8,4},{9,5},{10,6},{1... | collective-permute-start | bytes 196616 | tf_op jit(solution)/shard_map/ppermute | solution.py:489
  25.1 1.2 %shard_map.75.refs_0_ = f32[8,2,2,96,128]{4,3,2,1,0:T(8,128)S(1)} custom-call(s32[8]{0:T(128)S(1)} %copy-done.1, bf16[2,128,512]{2,1,0:T(8,128)(2,1)S(1)} %get-tuple-element.31.refs_0_, bf16[2,128,512]{2,1,0:T(8,128)(2,1)S(1)} %collective-permute-done.refs_1_, bf16[2,128,512]{2,1,0:T(8,128)(2,1)S(1)} %collective-permute-done.1.refs_2_, ...), custom_call_target="tpu_custom_call" | custom-call | flops 1000000000 | bytes 1048576 | tf_op jit(solution)/shard_map/pallas_call | solution.py:530
  26.3 1.6 %shard_map.76 = (bf16[328,128]{1,0:T(8,128)(2,1)S(1)}, bf16[328,128]{1,0:T(8,128)(2,1)S(1)}, bf16[328,128]{1,0:T(8,128)(2,1)S(1)}, bf16[328,128]{1,0:T(8,128)(2,...) custom-call(f32[8,2,2,96,128]{4,3,2,1,0:T(8,128)S(1)} %shard_map.75., ...), custom_call_target="tpu_custom_call" | custom-call | flops 4000000000 | bytes 1048576 | tf_op jit(solution)/shard_map/pallas_call | solution.py:542
  27.9 5.1 %collective-permute-start.18 = (bf16[328,128]{1,0:T(8,128)(2,1)S(1)}, bf16[328,128]{1,0:T(8,128)(2,1)S(1)}, u32[]{:S(2)}, u32[]{:S(2)}) collective-permute-start(bf16[328,128]{1,0:T(8,128)(2,1)S(1)} %get-tuple-element.55), channel_id=1, source_target_pairs={{0,28},{4,24},{8,20},{12,16},{16,12},{20,8},{24,4},{28,0},{1,29},{... | collective-permute-start | bytes 251912 | tf_op jit(solution)/shard_map/ppermute | solution.py:21
  34.9 2.2 %shard_map.77 = (bf16[528,128]{1,0:T(8,128)(2,1)S(1)}, bf16[528,128]{1,0:T(8,128)(2,1)S(1)}, bf16[528,128]{1,0:T(8,128)(2,1)S(1)}, bf16[528,128]{1,0:T(8,128)(2,...) custom-call(s32[8]{0:T(128)S(1)} %copy-done.1, ...), custom_call_target="tpu_custom_call" | custom-call | flops 4000000000 | bytes 1048576 | tf_op jit(solution)/shard_map/pallas_call | solution.py:542
  37.1 1.9 %collective-permute-start.15 = (bf16[528,128]{1,0:T(8,128)(2,1)S(1)}, bf16[528,128]{1,0:T(8,128)(2,1)S(1)}, u32[]{:S(2)}, u32[]{:S(2)}) collective-permute-start(bf16[528,128]{1,0:T(8,128)(2,1)S(1)} %get-tuple-element.51), channel_id=1, source_target_pairs={{0,20},{4,16},{8,28},{12,24},{16,4},{20,0},{24,12},{28,8},{1,21},{... | collective-permute-start | bytes 405512 | tf_op jit(solution)/shard_map/ppermute | solution.py:21
  39.0 2.6 %collective-permute-start.16 = (bf16[528,128]{1,0:T(8,128)(2,1)S(1)}, bf16[528,128]{1,0:T(8,128)(2,1)S(1)}, u32[]{:S(2)}, u32[]{:S(2)}) collective-permute-start(bf16[528,128]{1,0:T(8,128)(2,1)S(1)} %get-tuple-element.52), channel_id=1, source_target_pairs={{0,12},{4,8},{8,4},{12,0},{16,28},{20,24},{24,20},{28,16},{1,13},{... | collective-permute-start | bytes 405512 | tf_op jit(solution)/shard_map/ppermute | solution.py:21
  41.5 2.3 %collective-permute-start.17 = (bf16[528,128]{1,0:T(8,128)(2,1)S(1)}, bf16[528,128]{1,0:T(8,128)(2,1)S(1)}, u32[]{:S(2)}, u32[]{:S(2)}) collective-permute-start(bf16[528,128]{1,0:T(8,128)(2,1)S(1)} %get-tuple-element.53), channel_id=1, source_target_pairs={{0,4},{4,0},{8,12},{12,8},{16,20},{20,16},{24,28},{28,24},{1,5},{5... | collective-permute-start | bytes 405512 | tf_op jit(solution)/shard_map/ppermute | solution.py:21
  43.8 1.3 %shard_map.78 = (bf16[1,2,256,256]{3,2,1,0:T(8,128)(2,1)S(1)}, f32[8,2,2,128,256]{4,3,2,1,0:T(8,128)S(1)}) custom-call(bf16[32,256]{1,0:T(8,128)(2,1)S(1)} %get-tuple-element.48.refs_0_), custom_call_target="tpu_custom_call" | custom-call | flops 2000000000 | bytes 1048576 | tf_op jit(solution)/shard_map/pallas_call | solution.py:492
  45.7 1.1 %final.3.refs_5_ = bf16[2,1024,256]{2,1,0:T(8,128)(2,1)} custom-call(bf16[528,128]{1,0:T(8,128)(2,1)S(1)} %get-tuple-element.54.refs_0_, bf16[328,128]{1,0:T(8,128)(2,1)S(1)} %collective-permute-done.18.refs_1_, bf16[328,128]{1,0:T(8,128)(2,1)S(1)} %collective-permute-done.19.refs_2_, bf16[1,2,256,256]{3,2,1,0:T(8,128)(2,1)S(1)} %get-tuple-element.49.refs_3_.refs_4_, ...), custom_call_target="tpu_custom_call" | custom-call | flops 1000000000 | bytes 1048576 | tf_op jit(solution)/shard_map/final/pallas_call | solution.py:595
  46.9 5.7 %collective-permute-start.12 = (bf16[200,128]{1,0:T(8,128)(2,1)S(1)}, bf16[200,128]{1,0:T(8,128)(2,1)S(1)}, u32[]{:S(2)}, u32[]{:S(2)}) collective-permute-start(bf16[200,128]{1,0:T(8,128)(2,1)S(1)} %get-tuple-element.45), channel_id=1, source_target_pairs={{0,28},{4,24},{8,20},{12,16},{16,12},{20,8},{24,4},{28,0},{1,29},{... | collective-permute-start | bytes 153608 | tf_op jit(solution)/shard_map/ppermute | solution.py:21
  52.6 1.2 %final.4.refs_6_ = bf16[2,1024,256]{2,1,0:T(8,128)(2,1)} custom-call(bf16[528,128]{1,0:T(8,128)(2,1)S(1)} %collective-permute-done.15.refs_0_, bf16[528,128]{1,0:T(8,128)(2,1)S(1)} %collective-permute-done.16.refs_1_, bf16[528,128]{1,0:T(8,128)(2,1)S(1)} %collective-permute-done.17.refs_2_, ...), custom_call_target="tpu_custom_call", output_to_operand_aliasing={{}: (5, {})} | custom-call | flops 1000000000 | bytes 1048576 | tf_op jit(solution)/shard_map/final/pallas_call | solution.py:595
  53.8 2.3 %collective-permute-done.12.refs_1_ = bf16[200,128]{1,0:T(8,128)(2,1)S(1)} collective-permute-done((bf16[200,128]{1,0:T(8,128)(2,1)S(1)}, bf16[200,128]{1,0:T(8,128)(2,1)S(1)}, u32[]{:S(2)}, u32[]{:S(2)}) %collective-permute-start.12) | collective-permute-done | bytes 51232 | tf_op jit(solution)/shard_map/ppermute | solution.py:21
  56.1 2.4 %collective-permute-done.13.refs_2_ = bf16[200,128]{1,0:T(8,128)(2,1)S(1)} collective-permute-done((bf16[200,128]{1,0:T(8,128)(2,1)S(1)}, bf16[200,128]{1,0:T(8,128)(2,1)S(1)}, u32[]{:S(2)}, u32[]{:S(2)}) %collective-permute-start.13) | collective-permute-done | bytes 51232 | tf_op jit(solution)/shard_map/ppermute | solution.py:21
  58.5 1.2 %final.5 = bf16[2,1024,256]{2,1,0:T(8,128)(2,1)} custom-call(bf16[528,128]{1,0:T(8,128)(2,1)S(1)} %collective-permute-done.11.refs_0_, bf16[200,128]{1,0:T(8,128)(2,1)S(1)} %collective-permute-done.12.refs_1_, bf16[200,128]{1,0:T(8,128)(2,1)S(1)} %collective-permute-done.13.refs_2_, ...), custom_call_target="tpu_custom_call", output_to_operand_aliasing={{}: (6, {})} | custom-call | flops 1000000000 | bytes 1048576 | tf_op jit(solution)/shard_map/final/pallas_call | solution.py:595
  (35 shorter events, 4.5 us)
Async XLA Ops:
  1.4 23.7 %copy-start = (bf16[2,256,256]{2,1,0:T(8,128)(2,1)S(1)}, bf16[2,256,256]{2,1,0:T(8,128)(2,1)}, u32[]{:S(2)}) copy-start(bf16[2,256,256]{2,1,0:T(8,128)(2,1)} %refs_3_.1) | copy-start | bytes 786436
  1.4 23.7 %copy-start.1 = (s32[8]{0:T(128)S(1)}, s32[8]{0:T(128)}, u32[]{:S(2)}) copy-start(s32[8]{0:T(128)} %refs_0_.1) | copy-start | bytes 100
  1.5 8.1 %collective-permute-start.6 = (bf16[56,256]{1,0:T(8,128)(2,1)S(1)}, bf16[56,256]{1,0:T(8,128)(2,1)S(1)}, u32[]{:S(2)}, u32[]{:S(2)}) collective-permute-start(bf16[56,256]{1,0:T(8,128)(2,1)S(1)} %get-tuple-element.35.refs_0_), channel_id=1, source_target_pairs={{0,12},{1,9},{2,14},{3,11},{4,8},{5,13},{6,10},{7,15},{8,4},{9,1},... | collective-permute-start | bytes 86024 | tf_op jit(solution)/shard_map/ppermute | solution.py:460
  5.5 6.6 %collective-permute-start.4 = (bf16[56,256]{1,0:T(8,128)(2,1)S(1)}, bf16[56,256]{1,0:T(8,128)(2,1)S(1)}, u32[]{:S(2)}, u32[]{:S(2)}) collective-permute-start(bf16[56,256]{1,0:T(8,128)(2,1)S(1)} %get-tuple-element.35.refs_0_), channel_id=1, source_target_pairs={{0,28},{1,25},{2,30},{3,27},{4,24},{5,29},{6,26},{7,31},{8,20},{9,... | collective-permute-start | bytes 86024 | tf_op jit(solution)/shard_map/ppermute | solution.py:460
  7.9 6.0 %collective-permute-start.5 = (bf16[56,256]{1,0:T(8,128)(2,1)S(1)}, bf16[56,256]{1,0:T(8,128)(2,1)S(1)}, u32[]{:S(2)}, u32[]{:S(2)}) collective-permute-start(bf16[56,256]{1,0:T(8,128)(2,1)S(1)} %get-tuple-element.35.refs_0_), channel_id=1, source_target_pairs={{0,20},{1,17},{2,22},{3,19},{4,16},{5,21},{6,18},{7,23},{8,28},{9,... | collective-permute-start | bytes 86024 | tf_op jit(solution)/shard_map/ppermute | solution.py:460
  8.3 5.6 %collective-permute-start.7 = (bf16[56,256]{1,0:T(8,128)(2,1)S(1)}, bf16[56,256]{1,0:T(8,128)(2,1)S(1)}, u32[]{:S(2)}, u32[]{:S(2)}) collective-permute-start(bf16[56,256]{1,0:T(8,128)(2,1)S(1)} %get-tuple-element.35.refs_0_), channel_id=1, source_target_pairs={{0,4},{1,5},{2,6},{3,7},{4,0},{5,1},{6,2},{7,3},{8,12},{9,13},{10,... | collective-permute-start | bytes 86024 | tf_op jit(solution)/shard_map/ppermute | solution.py:460
  9.6 9.1 %collective-permute-start.2 = (bf16[2,128,512]{2,1,0:T(8,128)(2,1)S(1)}, bf16[2,128,512]{2,1,0:T(8,128)(2,1)S(1)}, u32[]{:S(2)}, u32[]{:S(2)}) collective-permute-start(bf16[2,128,512]{2,1,0:T(8,128)(2,1)S(1)} %get-tuple-element.34), channel_id=1, source_target_pairs={{0,3},{1,2},{2,1},{3,0},{4,7},{5,6},{6,5},{7,4},{8,11},{9,10},{10,... | collective-permute-start | bytes 786440 | tf_op jit(solution)/shard_map/ppermute | solution.py:21
  9.6 4.9 %collective-permute-start.10 = (bf16[56,256]{1,0:T(8,128)(2,1)S(1)}, bf16[56,256]{1,0:T(8,128)(2,1)S(1)}, u32[]{:S(2)}, u32[]{:S(2)}) collective-permute-start(bf16[56,256]{1,0:T(8,128)(2,1)S(1)} %collective-permute-done.6.refs_3_), channel_id=1, source_target_pairs={{0,1},{1,0},{2,3},{3,2},{4,5},{5,4},{6,7},{7,6},{8,9},{9,8},{10,11... | collective-permute-start | bytes 86024 | tf_op jit(solution)/shard_map/ppermute | solution.py:21
  12.1 3.9 %collective-permute-start.8 = (bf16[56,256]{1,0:T(8,128)(2,1)S(1)}, bf16[56,256]{1,0:T(8,128)(2,1)S(1)}, u32[]{:S(2)}, u32[]{:S(2)}) collective-permute-start(bf16[56,256]{1,0:T(8,128)(2,1)S(1)} %collective-permute-done.4.refs_1_), channel_id=1, source_target_pairs={{0,1},{1,0},{2,3},{3,2},{4,5},{5,4},{6,7},{7,6},{8,9},{9,8},{10,11... | collective-permute-start | bytes 86024 | tf_op jit(solution)/shard_map/ppermute | solution.py:21
  13.9 2.0 %collective-permute-start.9 = (bf16[56,256]{1,0:T(8,128)(2,1)S(1)}, bf16[56,256]{1,0:T(8,128)(2,1)S(1)}, u32[]{:S(2)}, u32[]{:S(2)}) collective-permute-start(bf16[56,256]{1,0:T(8,128)(2,1)S(1)} %collective-permute-done.5.refs_2_), channel_id=1, source_target_pairs={{0,1},{1,0},{2,3},{3,2},{4,5},{5,4},{6,7},{7,6},{8,9},{9,8},{10,11... | collective-permute-start | bytes 86024 | tf_op jit(solution)/shard_map/ppermute | solution.py:21
  13.9 9.9 %collective-permute-start = (bf16[2,128,512]{2,1,0:T(8,128)(2,1)S(1)}, bf16[2,128,512]{2,1,0:T(8,128)(2,1)S(1)}, u32[]{:S(2)}, u32[]{:S(2)}) collective-permute-start(bf16[2,128,512]{2,1,0:T(8,128)(2,1)S(1)} %get-tuple-element.32), channel_id=1, source_target_pairs={{0,1},{1,0},{2,3},{3,2},{4,5},{5,4},{6,7},{7,6},{8,9},{9,8},{10,11... | collective-permute-start | bytes 786440 | tf_op jit(solution)/shard_map/ppermute | solution.py:21
  14.4 9.3 %collective-permute-start.1 = (bf16[2,128,512]{2,1,0:T(8,128)(2,1)S(1)}, bf16[2,128,512]{2,1,0:T(8,128)(2,1)S(1)}, u32[]{:S(2)}, u32[]{:S(2)}) collective-permute-start(bf16[2,128,512]{2,1,0:T(8,128)(2,1)S(1)} %get-tuple-element.33), channel_id=1, source_target_pairs={{0,2},{1,3},{2,0},{3,1},{4,6},{5,7},{6,4},{7,5},{8,10},{9,11},{10,... | collective-permute-start | bytes 786440 | tf_op jit(solution)/shard_map/ppermute | solution.py:21
  23.8 11.1 %collective-permute-start.3 = (bf16[4,2,8,512]{3,2,1,0:T(8,128)(2,1)S(1)}, bf16[4,2,8,512]{3,2,1,0:T(8,128)(2,1)S(1)}, u32[]{:S(2)}, u32[]{:S(2)}) collective-permute-start(bf16[4,2,8,512]{3,2,1,0:T(8,128)(2,1)S(1)} %pad_maximum_fusion), channel_id=1, source_target_pairs={{1,28},{2,29},{3,30},{4,0},{5,1},{6,2},{7,3},{8,4},{9,5},{10,6},{1... | collective-permute-start | bytes 196616 | tf_op jit(solution)/shard_map/ppermute | solution.py:489
  27.9 17.2 %collective-permute-start.18 = (bf16[328,128]{1,0:T(8,128)(2,1)S(1)}, bf16[328,128]{1,0:T(8,128)(2,1)S(1)}, u32[]{:S(2)}, u32[]{:S(2)}) collective-permute-start(bf16[328,128]{1,0:T(8,128)(2,1)S(1)} %get-tuple-element.55), channel_id=1, source_target_pairs={{0,28},{4,24},{8,20},{12,16},{16,12},{20,8},{24,4},{28,0},{1,29},{... | collective-permute-start | bytes 251912 | tf_op jit(solution)/shard_map/ppermute | solution.py:21
  33.0 12.2 %collective-permute-start.19 = (bf16[328,128]{1,0:T(8,128)(2,1)S(1)}, bf16[328,128]{1,0:T(8,128)(2,1)S(1)}, u32[]{:S(2)}, u32[]{:S(2)}) collective-permute-start(bf16[328,128]{1,0:T(8,128)(2,1)S(1)} %get-tuple-element.56), channel_id=1, source_target_pairs={{0,24},{4,28},{8,16},{12,20},{16,8},{20,12},{24,0},{28,4},{1,25},{... | collective-permute-start | bytes 251912 | tf_op jit(solution)/shard_map/ppermute | solution.py:21
  37.1 9.8 %collective-permute-start.15 = (bf16[528,128]{1,0:T(8,128)(2,1)S(1)}, bf16[528,128]{1,0:T(8,128)(2,1)S(1)}, u32[]{:S(2)}, u32[]{:S(2)}) collective-permute-start(bf16[528,128]{1,0:T(8,128)(2,1)S(1)} %get-tuple-element.51), channel_id=1, source_target_pairs={{0,20},{4,16},{8,28},{12,24},{16,4},{20,0},{24,12},{28,8},{1,21},{... | collective-permute-start | bytes 405512 | tf_op jit(solution)/shard_map/ppermute | solution.py:21
  39.0 13.6 %collective-permute-start.16 = (bf16[528,128]{1,0:T(8,128)(2,1)S(1)}, bf16[528,128]{1,0:T(8,128)(2,1)S(1)}, u32[]{:S(2)}, u32[]{:S(2)}) collective-permute-start(bf16[528,128]{1,0:T(8,128)(2,1)S(1)} %get-tuple-element.52), channel_id=1, source_target_pairs={{0,12},{4,8},{8,4},{12,0},{16,28},{20,24},{24,20},{28,16},{1,13},{... | collective-permute-start | bytes 405512 | tf_op jit(solution)/shard_map/ppermute | solution.py:21
  41.5 11.1 %collective-permute-start.17 = (bf16[528,128]{1,0:T(8,128)(2,1)S(1)}, bf16[528,128]{1,0:T(8,128)(2,1)S(1)}, u32[]{:S(2)}, u32[]{:S(2)}) collective-permute-start(bf16[528,128]{1,0:T(8,128)(2,1)S(1)} %get-tuple-element.53), channel_id=1, source_target_pairs={{0,4},{4,0},{8,12},{12,8},{16,20},{20,16},{24,28},{28,24},{1,5},{5... | collective-permute-start | bytes 405512 | tf_op jit(solution)/shard_map/ppermute | solution.py:21
  45.1 13.4 %collective-permute-start.11 = (bf16[528,128]{1,0:T(8,128)(2,1)S(1)}, bf16[528,128]{1,0:T(8,128)(2,1)S(1)}, u32[]{:S(2)}, u32[]{:S(2)}) collective-permute-start(bf16[528,128]{1,0:T(8,128)(2,1)S(1)} %get-tuple-element.44), channel_id=1, source_target_pairs={{0,16},{4,20},{8,24},{12,28},{16,0},{20,4},{24,8},{28,12},{1,17},{... | collective-permute-start | bytes 405512 | tf_op jit(solution)/shard_map/ppermute | solution.py:21
  45.2 13.4 %collective-permute-start.14 = (bf16[528,128]{1,0:T(8,128)(2,1)S(1)}, bf16[528,128]{1,0:T(8,128)(2,1)S(1)}, u32[]{:S(2)}, u32[]{:S(2)}) collective-permute-start(bf16[528,128]{1,0:T(8,128)(2,1)S(1)} %get-tuple-element.47), channel_id=1, source_target_pairs={{0,8},{4,12},{8,0},{12,4},{16,24},{20,28},{24,16},{28,20},{1,9},{5... | collective-permute-start | bytes 405512 | tf_op jit(solution)/shard_map/ppermute | solution.py:21
  46.9 9.2 %collective-permute-start.12 = (bf16[200,128]{1,0:T(8,128)(2,1)S(1)}, bf16[200,128]{1,0:T(8,128)(2,1)S(1)}, u32[]{:S(2)}, u32[]{:S(2)}) collective-permute-start(bf16[200,128]{1,0:T(8,128)(2,1)S(1)} %get-tuple-element.45), channel_id=1, source_target_pairs={{0,28},{4,24},{8,20},{12,16},{16,12},{20,8},{24,4},{28,0},{1,29},{... | collective-permute-start | bytes 153608 | tf_op jit(solution)/shard_map/ppermute | solution.py:21
  52.6 5.9 %collective-permute-start.13 = (bf16[200,128]{1,0:T(8,128)(2,1)S(1)}, bf16[200,128]{1,0:T(8,128)(2,1)S(1)}, u32[]{:S(2)}, u32[]{:S(2)}) collective-permute-start(bf16[200,128]{1,0:T(8,128)(2,1)S(1)} %get-tuple-element.46), channel_id=1, source_target_pairs={{0,24},{4,28},{8,16},{12,20},{16,8},{20,12},{24,0},{28,4},{1,25},{... | collective-permute-start | bytes 153608 | tf_op jit(solution)/shard_map/ppermute | solution.py:21

commit v3 on v2

--- a/solution.py
+++ b/solution.py
@@ -224,9 +224,8 @@
     return place
 
 
-def form_kernel(group, pulse_count, sources, first, count, sub_map, *refs):
-    blocks, steering, image = refs[:sources], refs[sources], refs[sources + 1]
-    half = image.shape[-1]
+def form_rows(group, pulse_count, sources, first, sub_map, blocks, steering, image):
+    half, count = image.shape[-1], image.shape[-2]
     per_source = group // sources
     slab = lax.axis_index("rng")
     for source in range(sources):
@@ -272,15 +271,18 @@
     return jnp.dot(jnp.concatenate(pieces, axis=0), matrix, preferred_element_type=jnp.float32)
 
 
-def merge_kernel(group, segments, chunk, first, rows, whole, pulse_count, sources, *refs):
-    if chunk == 0:
-        image, bands, waves = refs[:3]
-        refs = refs[3:]
-    else:
-        sub_map, image, edge, steering, bands, waves = refs[:6]
-        kept, refs = dict(zip(whole, refs[6:])), refs[6 + len(whole) :]
-        edges, refs = refs[group], refs[:group] + refs[group + 1 :]
-    outs, stores = refs[:group], refs[group:]
+def merge_kernel(
+    group, segments, chunk, first, rows, whole, pulse_count, sources, sub_map, *refs
+):
+    blocks, refs = refs[:sources], refs[sources:]
+    steering, bands, waves, refs = refs[0], refs[1], refs[2], refs[3:]
+    if chunk == 1:
+        edge, kept, refs = refs[0], dict(zip(whole, refs[1:])), refs[1 + len(whole) :]
+    outs, image, refs = refs[:group], refs[group], refs[group + 1 :]
+    if chunk == 1:
+        edges, refs = refs[0], refs[1:]
+    stores = refs
+    form_rows(group, pulse_count, sources, first, sub_map, blocks, steering, image)
     half = image.shape[-1]
     member = lax.axis_index("sub") & (group - 1)
     per_source = group // sources
@@ -526,19 +528,12 @@
     split = [mask for mask, _ in upper_order]
     whole_masks = [mask for mask in range(group) if mask not in split]
 
-    def form(first, count):
-        return pl.pallas_call(
-            functools.partial(form_kernel, group, pulse_count, len(blocks), first, count),
-            out_shape=jax.ShapeDtypeStruct((group, 2, 2, count, half), jnp.float32),
-            in_specs=[SCALARS] + [WHOLE] * (len(blocks) + 1),
-            out_specs=WHOLE,
-            compiler_params=params(6),
-            cost_estimate=cost(1_000_000_000),
-        )(sub_map, *blocks, steering)
-
     def merge(chunk, arrays, sizes):
         first, count = bounds[chunk]
-        edges = [pltpu.VMEM((group, 2, 2, 16, half), jnp.float32)] if chunk == 1 else []
+        held = count if chunk == 1 else count + 16
+        scratch = [pltpu.VMEM((group, 2, 2, held, half), jnp.float32)]
+        if chunk == 1:
+            scratch.append(pltpu.VMEM((group, 2, 2, 16, half), jnp.float32))
         return pl.pallas_call(
             functools.partial(
                 merge_kernel,
@@ -552,26 +547,25 @@
                 len(blocks),
             ),
             out_shape=[jax.ShapeDtypeStruct((size, half), jnp.bfloat16) for size in sizes],
-            in_specs=([SCALARS] if chunk == 1 else []) + [WHOLE] * (len(arrays) - chunk),
+            in_specs=[SCALARS] + [WHOLE] * (len(blocks) + 3 + len(arrays)),
             out_specs=[WHOLE] * group,
-            scratch_shapes=edges
+            scratch_shapes=scratch
             + [pltpu.VMEM((group, 2, 2, count + 16, half), jnp.float32)] * (segments - 1),
-            compiler_params=params(8),
+            compiler_params=params(10),
             cost_estimate=cost(4_000_000_000),
-        )(*arrays)
+        )(sub_map, *blocks, steering, bands, waves, *arrays)
 
     arrived = {}
 
     def send(mask, chunk, value):
         arrived[mask, chunk] = exchanged(value, "sub", mask)
 
-    upper = merge(0, [form(0, cut_row + 16), bands, waves], pieces[:1] * group)
+    upper = merge(0, [], pieces[:1] * group)
     for mask, chunk in upper_order:
         send(mask, chunk, upper[mask])
     lower = merge(
         1,
-        [sub_map, form(*bounds[1]), edge, steering, bands, waves]
-        + [upper[mask] for mask in whole_masks],
+        [edge] + [upper[mask] for mask in whole_masks],
         [sum(pieces) if mask in whole_masks else pieces[1] for mask in range(group)],
     )
     for mask, chunk in lower_order:

time: 59.9 us -> 58.4 us (0.975)
  the two profiles are of different devices: /device:TPU:0 before, /device:TPU:4 now
where the time goes in v3:
time: 58.4 us; the launch traced here: 58.2 us
  starting transfers between devices  31.6 us (54%)
  Pallas kernels  14.1 us (24%)
  waiting for transfers between devices  12.3 us (21%)
    ppermute x15, starting transfers between devices, exchanged(): lax.ppermute(block, axis, [(source, source ^ mask) for source in range(co...  17.7 us
    ppermute x15, waiting for transfers between devices, exchanged(): lax.ppermute(block, axis, [(source, source ^ mask) for source in range(co...  9.27 us
    ppermute x1, starting transfers between devices, on_device(): edge = lax.ppermute(edge_rows, ('sub', 'rng'), route)  7.09 us
    ppermute x4, starting transfers between devices, on_device(): mine.append(lax.ppermute(early_pack, ('sub', 'rng'), route))  6.81 us
    pallas_call x2, Pallas kernels, merge(): pl.pallas_call(functools.partial(merge_kernel, group, segments, chunk, fi...  5.29 us
    pallas_call x2, Pallas kernels, tables(): pl.pallas_call(functools.partial(table_kernel, group, terms, sources, tap...  3.98 us
    pallas_call x3, Pallas kernels, on_device(): pl.pallas_call(functools.partial(final_kernel, jobs, count, group, rows,...  3.42 us
    ppermute x4, waiting for transfers between devices, on_device(): mine.append(lax.ppermute(early_pack, ('sub', 'rng'), route))  3.05 us
  transfers between devices with their start and end apart: 20, of which 6 were waited for; matrix products, arithmetic and copies ran while one was open for 0% of the time, Pallas kernels for 20%

profile of v3, /device:TPU:4, one launch (start us, length us, event | category | flops | bytes accessed | tf_op | source)
XLA Modules:
  0.0 58.2 jit_solution(8317540190253017240)
XLA Ops:
  0.0 1.4 %cut.1 = (bf16[2,128,512]{2,1,0:T(8,128)(2,1)S(1)}, bf16[2,128,512]{2,1,0:T(8,128)(2,1)S(1)}, bf16[2,128,512]{2,1,0:T(8,128)(2,1)S(1)}, bf16[2,128,512]{2,1,0:T(...) custom-call(bf16[2,4,128,512]{3,2,1,0:T(8,128)(2,1)} %echoes.1, s32[1,3,2,256]{3,2,1,0:T(2,128)} %offset.1, ...), custom_call_target="tpu_custom_call" | custom-call | flops 1000000000 | bytes 1048576 | tf_op jit(solution)/shard_map/cut/pallas_call | solution.py:437
  1.5 4.6 %collective-permute-start.3 = (bf16[56,256]{1,0:T(8,128)(2,1)S(1)}, bf16[56,256]{1,0:T(8,128)(2,1)S(1)}, u32[]{:S(2)}, u32[]{:S(2)}) collective-permute-start(bf16[56,256]{1,0:T(8,128)(2,1)S(1)} %get-tuple-element.35.refs_0_), channel_id=1, source_target_pairs={{0,28},{1,25},{2,30},{3,27},{4,24},{5,29},{6,26},{7,31},{8,20},{9,... | collective-permute-start | bytes 86024 | tf_op jit(solution)/shard_map/ppermute | solution.py:462
  6.0 1.7 %collective-permute-start.5 = (bf16[56,256]{1,0:T(8,128)(2,1)S(1)}, bf16[56,256]{1,0:T(8,128)(2,1)S(1)}, u32[]{:S(2)}, u32[]{:S(2)}) collective-permute-start(bf16[56,256]{1,0:T(8,128)(2,1)S(1)} %get-tuple-element.35.refs_0_), channel_id=1, source_target_pairs={{0,12},{1,9},{2,14},{3,11},{4,8},{5,13},{6,10},{7,15},{8,4},{9,1},... | collective-permute-start | bytes 86024 | tf_op jit(solution)/shard_map/ppermute | solution.py:462
  7.7 0.5 collective-permute-start.6
  8.8 3.0 %collective-permute-done.4.refs_2_ = bf16[56,256]{1,0:T(8,128)(2,1)S(1)} collective-permute-done((bf16[56,256]{1,0:T(8,128)(2,1)S(1)}, bf16[56,256]{1,0:T(8,128)(2,1)S(1)}, u32[]{:S(2)}, u32[]{:S(2)}) %collective-permute-start.4) | collective-permute-done | bytes 28704 | tf_op jit(solution)/shard_map/ppermute | solution.py:462
  11.8 0.5 collective-permute-start.9
  12.4 0.5 collective-permute-start.1
  13.2 2.7 %shard_map.73 = (bf16[8,4,256,256]{3,2,1,0:T(8,128)(2,1)S(1)}, f32[8,4,2,136,256]{4,3,2,1,0:T(8,128)S(1)}) custom-call(bf16[56,256]{1,0:T(8,128)(2,1)S(1)} %get-tuple-element.35.refs_0_, bf16[56,256]{1,0:T(8,128)(2,1)S(1)} %collective-permute-done.3.refs_1_, bf16[56,256]{1,0:T(8,128)(2,1)S(1)} %collective-permute-done.4.refs_2_, ...), custom_call_target="tpu_custom_call" | custom-call | flops 2000000000 | bytes 1048576 | tf_op jit(solution)/shard_map/pallas_call | solution.py:494
  15.9 5.5 %collective-permute-done.1.refs_2_ = bf16[2,128,512]{2,1,0:T(8,128)(2,1)S(1)} collective-permute-done((bf16[2,128,512]{2,1,0:T(8,128)(2,1)S(1)}, bf16[2,128,512]{2,1,0:T(8,128)(2,1)S(1)}, u32[]{:S(2)}, u32[]{:S(2)}) %collective-permute-start.1) | collective-permute-done | bytes 262176 | tf_op jit(solution)/shard_map/ppermute | solution.py:21
  21.5 7.1 %collective-permute-start.10 = (bf16[4,2,8,512]{3,2,1,0:T(8,128)(2,1)S(1)}, bf16[4,2,8,512]{3,2,1,0:T(8,128)(2,1)S(1)}, u32[]{:S(2)}, u32[]{:S(2)}) collective-permute-start(bf16[4,2,8,512]{3,2,1,0:T(8,128)(2,1)S(1)} %pad_maximum_fusion), channel_id=1, source_target_pairs={{1,28},{2,29},{3,30},{4,0},{5,1},{6,2},{7,3},{8,4},{9,5},{10,6},{1... | collective-permute-start | bytes 196616 | tf_op jit(solution)/shard_map/ppermute | solution.py:491
  28.6 2.8 %shard_map.74 = (bf16[328,128]{1,0:T(8,128)(2,1)S(1)}, bf16[328,128]{1,0:T(8,128)(2,1)S(1)}, bf16[328,128]{1,0:T(8,128)(2,1)S(1)}, bf16[328,128]{1,0:T(8,128)(2,...) custom-call(s32[8]{0:T(128)S(1)} %copy-done.1, ...), custom_call_target="tpu_custom_call" | custom-call | flops 4000000000 | bytes 1048576 | tf_op jit(solution)/shard_map/pallas_call | solution.py:537
  31.6 2.5 %shard_map.75 = (bf16[528,128]{1,0:T(8,128)(2,1)S(1)}, bf16[528,128]{1,0:T(8,128)(2,1)S(1)}, bf16[528,128]{1,0:T(8,128)(2,1)S(1)}, bf16[528,128]{1,0:T(8,128)(2,...) custom-call(s32[8]{0:T(128)S(1)} %copy-done.1, ...), custom_call_target="tpu_custom_call" | custom-call | flops 4000000000 | bytes 1048576 | tf_op jit(solution)/shard_map/pallas_call | solution.py:537
  34.1 5.2 %collective-permute-start.16 = (bf16[528,128]{1,0:T(8,128)(2,1)S(1)}, bf16[528,128]{1,0:T(8,128)(2,1)S(1)}, u32[]{:S(2)}, u32[]{:S(2)}) collective-permute-start(bf16[528,128]{1,0:T(8,128)(2,1)S(1)} %get-tuple-element.52), channel_id=1, source_target_pairs={{0,12},{4,8},{8,4},{12,0},{16,28},{20,24},{24,20},{28,16},{1,13},{... | collective-permute-start | bytes 405512 | tf_op jit(solution)/shard_map/ppermute | solution.py:21
  39.4 1.4 %collective-permute-start.17 = (bf16[528,128]{1,0:T(8,128)(2,1)S(1)}, bf16[528,128]{1,0:T(8,128)(2,1)S(1)}, u32[]{:S(2)}, u32[]{:S(2)}) collective-permute-start(bf16[528,128]{1,0:T(8,128)(2,1)S(1)} %get-tuple-element.53), channel_id=1, source_target_pairs={{0,4},{4,0},{8,12},{12,8},{16,20},{20,16},{24,28},{28,24},{1,5},{5... | collective-permute-start | bytes 405512 | tf_op jit(solution)/shard_map/ppermute | solution.py:21
  40.8 1.3 %shard_map.76 = (bf16[1,2,256,256]{3,2,1,0:T(8,128)(2,1)S(1)}, f32[8,2,2,128,256]{4,3,2,1,0:T(8,128)S(1)}) custom-call(bf16[32,256]{1,0:T(8,128)(2,1)S(1)} %get-tuple-element.48.refs_0_), custom_call_target="tpu_custom_call" | custom-call | flops 2000000000 | bytes 1048576 | tf_op jit(solution)/shard_map/pallas_call | solution.py:494
  42.1 1.0 %collective-permute-start.11 = (bf16[528,128]{1,0:T(8,128)(2,1)S(1)}, bf16[528,128]{1,0:T(8,128)(2,1)S(1)}, u32[]{:S(2)}, u32[]{:S(2)}) collective-permute-start(bf16[528,128]{1,0:T(8,128)(2,1)S(1)} %get-tuple-element.44), channel_id=1, source_target_pairs={{0,16},{4,20},{8,24},{12,28},{16,0},{20,4},{24,8},{28,12},{1,17},{... | collective-permute-start | bytes 405512 | tf_op jit(solution)/shard_map/ppermute | solution.py:21
  43.0 3.5 %collective-permute-start.14 = (bf16[528,128]{1,0:T(8,128)(2,1)S(1)}, bf16[528,128]{1,0:T(8,128)(2,1)S(1)}, u32[]{:S(2)}, u32[]{:S(2)}) collective-permute-start(bf16[528,128]{1,0:T(8,128)(2,1)S(1)} %get-tuple-element.47), channel_id=1, source_target_pairs={{0,8},{4,12},{8,0},{12,4},{16,24},{20,28},{24,16},{28,20},{1,9},{5... | collective-permute-start | bytes 405512 | tf_op jit(solution)/shard_map/ppermute | solution.py:21
  46.5 1.1 %final.3.refs_5_ = bf16[2,1024,256]{2,1,0:T(8,128)(2,1)} custom-call(bf16[528,128]{1,0:T(8,128)(2,1)S(1)} %get-tuple-element.54.refs_0_, bf16[328,128]{1,0:T(8,128)(2,1)S(1)} %collective-permute-done.18.refs_1_, bf16[328,128]{1,0:T(8,128)(2,1)S(1)} %collective-permute-done.19.refs_2_, bf16[1,2,256,256]{3,2,1,0:T(8,128)(2,1)S(1)} %get-tuple-element.49.refs_3_.refs_4_, ...), custom_call_target="tpu_custom_call" | custom-call | flops 1000000000 | bytes 1048576 | tf_op jit(solution)/shard_map/final/pallas_call | solution.py:589
  47.6 3.5 %collective-permute-start.12 = (bf16[200,128]{1,0:T(8,128)(2,1)S(1)}, bf16[200,128]{1,0:T(8,128)(2,1)S(1)}, u32[]{:S(2)}, u32[]{:S(2)}) collective-permute-start(bf16[200,128]{1,0:T(8,128)(2,1)S(1)} %get-tuple-element.45), channel_id=1, source_target_pairs={{0,28},{4,24},{8,20},{12,16},{16,12},{20,8},{24,4},{28,0},{1,29},{... | collective-permute-start | bytes 153608 | tf_op jit(solution)/shard_map/ppermute | solution.py:21
  51.1 1.3 %collective-permute-start.13 = (bf16[200,128]{1,0:T(8,128)(2,1)S(1)}, bf16[200,128]{1,0:T(8,128)(2,1)S(1)}, u32[]{:S(2)}, u32[]{:S(2)}) collective-permute-start(bf16[200,128]{1,0:T(8,128)(2,1)S(1)} %get-tuple-element.46), channel_id=1, source_target_pairs={{0,24},{4,28},{8,16},{12,20},{16,8},{20,12},{24,0},{28,4},{1,25},{... | collective-permute-start | bytes 153608 | tf_op jit(solution)/shard_map/ppermute | solution.py:21
  52.3 1.2 %final.4.refs_6_ = bf16[2,1024,256]{2,1,0:T(8,128)(2,1)} custom-call(bf16[528,128]{1,0:T(8,128)(2,1)S(1)} %collective-permute-done.15.refs_0_, bf16[528,128]{1,0:T(8,128)(2,1)S(1)} %collective-permute-done.16.refs_1_, bf16[528,128]{1,0:T(8,128)(2,1)S(1)} %collective-permute-done.17.refs_2_, ...), custom_call_target="tpu_custom_call", output_to_operand_aliasing={{}: (5, {})} | custom-call | flops 1000000000 | bytes 1048576 | tf_op jit(solution)/shard_map/final/pallas_call | solution.py:589
  53.5 1.3 %collective-permute-done.12.refs_1_ = bf16[200,128]{1,0:T(8,128)(2,1)S(1)} collective-permute-done((bf16[200,128]{1,0:T(8,128)(2,1)S(1)}, bf16[200,128]{1,0:T(8,128)(2,1)S(1)}, u32[]{:S(2)}, u32[]{:S(2)}) %collective-permute-start.12) | collective-permute-done | bytes 51232 | tf_op jit(solution)/shard_map/ppermute | solution.py:21
  54.8 2.2 %collective-permute-done.13.refs_2_ = bf16[200,128]{1,0:T(8,128)(2,1)S(1)} collective-permute-done((bf16[200,128]{1,0:T(8,128)(2,1)S(1)}, bf16[200,128]{1,0:T(8,128)(2,1)S(1)}, u32[]{:S(2)}, u32[]{:S(2)}) %collective-permute-start.13) | collective-permute-done | bytes 51232 | tf_op jit(solution)/shard_map/ppermute | solution.py:21
  57.0 1.2 %final.5 = bf16[2,1024,256]{2,1,0:T(8,128)(2,1)} custom-call(bf16[528,128]{1,0:T(8,128)(2,1)S(1)} %collective-permute-done.11.refs_0_, bf16[200,128]{1,0:T(8,128)(2,1)S(1)} %collective-permute-done.12.refs_1_, bf16[200,128]{1,0:T(8,128)(2,1)S(1)} %collective-permute-done.13.refs_2_, ...), custom_call_target="tpu_custom_call", output_to_operand_aliasing={{}: (6, {})} | custom-call | flops 1000000000 | bytes 1048576 | tf_op jit(solution)/shard_map/final/pallas_call | solution.py:589
  (33 shorter events, 1.2 us)
Async XLA Ops:
  1.4 27.1 %copy-start = (bf16[2,256,256]{2,1,0:T(8,128)(2,1)S(1)}, bf16[2,256,256]{2,1,0:T(8,128)(2,1)}, u32[]{:S(2)}) copy-start(bf16[2,256,256]{2,1,0:T(8,128)(2,1)} %refs_4_.3) | copy-start | bytes 786436
  1.4 27.1 %copy-start.1 = (s32[8]{0:T(128)S(1)}, s32[8]{0:T(128)}, u32[]{:S(2)}) copy-start(s32[8]{0:T(128)} %sub_map.3) | copy-start | bytes 100
  1.5 6.8 %collective-permute-start.3 = (bf16[56,256]{1,0:T(8,128)(2,1)S(1)}, bf16[56,256]{1,0:T(8,128)(2,1)S(1)}, u32[]{:S(2)}, u32[]{:S(2)}) collective-permute-start(bf16[56,256]{1,0:T(8,128)(2,1)S(1)} %get-tuple-element.35.refs_0_), channel_id=1, source_target_pairs={{0,28},{1,25},{2,30},{3,27},{4,24},{5,29},{6,26},{7,31},{8,20},{9,... | collective-permute-start | bytes 86024 | tf_op jit(solution)/shard_map/ppermute | solution.py:462
  6.0 5.8 %collective-permute-start.4 = (bf16[56,256]{1,0:T(8,128)(2,1)S(1)}, bf16[56,256]{1,0:T(8,128)(2,1)S(1)}, u32[]{:S(2)}, u32[]{:S(2)}) collective-permute-start(bf16[56,256]{1,0:T(8,128)(2,1)S(1)} %get-tuple-element.35.refs_0_), channel_id=1, source_target_pairs={{0,20},{1,17},{2,22},{3,19},{4,16},{5,21},{6,18},{7,23},{8,28},{9,... | collective-permute-start | bytes 86024 | tf_op jit(solution)/shard_map/ppermute | solution.py:462
  6.0 5.8 %collective-permute-start.5 = (bf16[56,256]{1,0:T(8,128)(2,1)S(1)}, bf16[56,256]{1,0:T(8,128)(2,1)S(1)}, u32[]{:S(2)}, u32[]{:S(2)}) collective-permute-start(bf16[56,256]{1,0:T(8,128)(2,1)S(1)} %get-tuple-element.35.refs_0_), channel_id=1, source_target_pairs={{0,12},{1,9},{2,14},{3,11},{4,8},{5,13},{6,10},{7,15},{8,4},{9,1},... | collective-permute-start | bytes 86024 | tf_op jit(solution)/shard_map/ppermute | solution.py:462
  7.7 4.6 %collective-permute-start.6 = (bf16[56,256]{1,0:T(8,128)(2,1)S(1)}, bf16[56,256]{1,0:T(8,128)(2,1)S(1)}, u32[]{:S(2)}, u32[]{:S(2)}) collective-permute-start(bf16[56,256]{1,0:T(8,128)(2,1)S(1)} %get-tuple-element.35.refs_0_), channel_id=1, source_target_pairs={{0,4},{1,5},{2,6},{3,7},{4,0},{5,1},{6,2},{7,3},{8,12},{9,13},{10,... | collective-permute-start | bytes 86024 | tf_op jit(solution)/shard_map/ppermute | solution.py:462
  8.3 7.6 %collective-permute-start.2 = (bf16[2,128,512]{2,1,0:T(8,128)(2,1)S(1)}, bf16[2,128,512]{2,1,0:T(8,128)(2,1)S(1)}, u32[]{:S(2)}, u32[]{:S(2)}) collective-permute-start(bf16[2,128,512]{2,1,0:T(8,128)(2,1)S(1)} %get-tuple-element.34), channel_id=1, source_target_pairs={{0,3},{1,2},{2,1},{3,0},{4,7},{5,6},{6,5},{7,4},{8,11},{9,10},{10,... | collective-permute-start | bytes 786440 | tf_op jit(solution)/shard_map/ppermute | solution.py:21
  8.3 4.1 %collective-permute-start.7 = (bf16[56,256]{1,0:T(8,128)(2,1)S(1)}, bf16[56,256]{1,0:T(8,128)(2,1)S(1)}, u32[]{:S(2)}, u32[]{:S(2)}) collective-permute-start(bf16[56,256]{1,0:T(8,128)(2,1)S(1)} %collective-permute-done.3.refs_1_), channel_id=1, source_target_pairs={{0,1},{1,0},{2,3},{3,2},{4,5},{5,4},{6,7},{7,6},{8,9},{9,8},{10,11... | collective-permute-start | bytes 86024 | tf_op jit(solution)/shard_map/ppermute | solution.py:21
  11.8 1.2 %collective-permute-start.8 = (bf16[56,256]{1,0:T(8,128)(2,1)S(1)}, bf16[56,256]{1,0:T(8,128)(2,1)S(1)}, u32[]{:S(2)}, u32[]{:S(2)}) collective-permute-start(bf16[56,256]{1,0:T(8,128)(2,1)S(1)} %collective-permute-done.4.refs_2_), channel_id=1, source_target_pairs={{0,1},{1,0},{2,3},{3,2},{4,5},{5,4},{6,7},{7,6},{8,9},{9,8},{10,11... | collective-permute-start | bytes 86024 | tf_op jit(solution)/shard_map/ppermute | solution.py:21
  11.8 1.4 %collective-permute-start.9 = (bf16[56,256]{1,0:T(8,128)(2,1)S(1)}, bf16[56,256]{1,0:T(8,128)(2,1)S(1)}, u32[]{:S(2)}, u32[]{:S(2)}) collective-permute-start(bf16[56,256]{1,0:T(8,128)(2,1)S(1)} %collective-permute-done.5.refs_3_), channel_id=1, source_target_pairs={{0,1},{1,0},{2,3},{3,2},{4,5},{5,4},{6,7},{7,6},{8,9},{9,8},{10,11... | collective-permute-start | bytes 86024 | tf_op jit(solution)/shard_map/ppermute | solution.py:21
  12.3 9.1 %collective-permute-start = (bf16[2,128,512]{2,1,0:T(8,128)(2,1)S(1)}, bf16[2,128,512]{2,1,0:T(8,128)(2,1)S(1)}, u32[]{:S(2)}, u32[]{:S(2)}) collective-permute-start(bf16[2,128,512]{2,1,0:T(8,128)(2,1)S(1)} %get-tuple-element.32), channel_id=1, source_target_pairs={{0,1},{1,0},{2,3},{3,2},{4,5},{5,4},{6,7},{7,6},{8,9},{9,8},{10,11... | collective-permute-start | bytes 786440 | tf_op jit(solution)/shard_map/ppermute | solution.py:21
  12.4 9.0 %collective-permute-start.1 = (bf16[2,128,512]{2,1,0:T(8,128)(2,1)S(1)}, bf16[2,128,512]{2,1,0:T(8,128)(2,1)S(1)}, u32[]{:S(2)}, u32[]{:S(2)}) collective-permute-start(bf16[2,128,512]{2,1,0:T(8,128)(2,1)S(1)} %get-tuple-element.33), channel_id=1, source_target_pairs={{0,2},{1,3},{2,0},{3,1},{4,6},{5,7},{6,4},{7,5},{8,10},{9,11},{10,... | collective-permute-start | bytes 786440 | tf_op jit(solution)/shard_map/ppermute | solution.py:21
  21.5 10.1 %collective-permute-start.10 = (bf16[4,2,8,512]{3,2,1,0:T(8,128)(2,1)S(1)}, bf16[4,2,8,512]{3,2,1,0:T(8,128)(2,1)S(1)}, u32[]{:S(2)}, u32[]{:S(2)}) collective-permute-start(bf16[4,2,8,512]{3,2,1,0:T(8,128)(2,1)S(1)} %pad_maximum_fusion), channel_id=1, source_target_pairs={{1,28},{2,29},{3,30},{4,0},{5,1},{6,2},{7,3},{8,4},{9,5},{10,6},{1... | collective-permute-start | bytes 196616 | tf_op jit(solution)/shard_map/ppermute | solution.py:491
  31.4 10.7 %collective-permute-start.18 = (bf16[328,128]{1,0:T(8,128)(2,1)S(1)}, bf16[328,128]{1,0:T(8,128)(2,1)S(1)}, u32[]{:S(2)}, u32[]{:S(2)}) collective-permute-start(bf16[328,128]{1,0:T(8,128)(2,1)S(1)} %get-tuple-element.55), channel_id=1, source_target_pairs={{0,28},{4,24},{8,20},{12,16},{16,12},{20,8},{24,4},{28,0},{1,29},{... | collective-permute-start | bytes 251912 | tf_op jit(solution)/shard_map/ppermute | solution.py:21
  31.5 11.6 %collective-permute-start.19 = (bf16[328,128]{1,0:T(8,128)(2,1)S(1)}, bf16[328,128]{1,0:T(8,128)(2,1)S(1)}, u32[]{:S(2)}, u32[]{:S(2)}) collective-permute-start(bf16[328,128]{1,0:T(8,128)(2,1)S(1)} %get-tuple-element.56), channel_id=1, source_target_pairs={{0,24},{4,28},{8,16},{12,20},{16,8},{20,12},{24,0},{28,4},{1,25},{... | collective-permute-start | bytes 251912 | tf_op jit(solution)/shard_map/ppermute | solution.py:21
  34.1 13.5 %collective-permute-start.15 = (bf16[528,128]{1,0:T(8,128)(2,1)S(1)}, bf16[528,128]{1,0:T(8,128)(2,1)S(1)}, u32[]{:S(2)}, u32[]{:S(2)}) collective-permute-start(bf16[528,128]{1,0:T(8,128)(2,1)S(1)} %get-tuple-element.51), channel_id=1, source_target_pairs={{0,20},{4,16},{8,28},{12,24},{16,4},{20,0},{24,12},{28,8},{1,21},{... | collective-permute-start | bytes 405512 | tf_op jit(solution)/shard_map/ppermute | solution.py:21
  34.1 16.9 %collective-permute-start.16 = (bf16[528,128]{1,0:T(8,128)(2,1)S(1)}, bf16[528,128]{1,0:T(8,128)(2,1)S(1)}, u32[]{:S(2)}, u32[]{:S(2)}) collective-permute-start(bf16[528,128]{1,0:T(8,128)(2,1)S(1)} %get-tuple-element.52), channel_id=1, source_target_pairs={{0,12},{4,8},{8,4},{12,0},{16,28},{20,24},{24,20},{28,16},{1,13},{... | collective-permute-start | bytes 405512 | tf_op jit(solution)/shard_map/ppermute | solution.py:21
  39.4 13.0 %collective-permute-start.17 = (bf16[528,128]{1,0:T(8,128)(2,1)S(1)}, bf16[528,128]{1,0:T(8,128)(2,1)S(1)}, u32[]{:S(2)}, u32[]{:S(2)}) collective-permute-start(bf16[528,128]{1,0:T(8,128)(2,1)S(1)} %get-tuple-element.53), channel_id=1, source_target_pairs={{0,4},{4,0},{8,12},{12,8},{16,20},{20,16},{24,28},{28,24},{1,5},{5... | collective-permute-start | bytes 405512 | tf_op jit(solution)/shard_map/ppermute | solution.py:21
  42.1 14.9 %collective-permute-start.11 = (bf16[528,128]{1,0:T(8,128)(2,1)S(1)}, bf16[528,128]{1,0:T(8,128)(2,1)S(1)}, u32[]{:S(2)}, u32[]{:S(2)}) collective-permute-start(bf16[528,128]{1,0:T(8,128)(2,1)S(1)} %get-tuple-element.44), channel_id=1, source_target_pairs={{0,16},{4,20},{8,24},{12,28},{16,0},{20,4},{24,8},{28,12},{1,17},{... | collective-permute-start | bytes 405512 | tf_op jit(solution)/shard_map/ppermute | solution.py:21
  43.0 13.9 %collective-permute-start.14 = (bf16[528,128]{1,0:T(8,128)(2,1)S(1)}, bf16[528,128]{1,0:T(8,128)(2,1)S(1)}, u32[]{:S(2)}, u32[]{:S(2)}) collective-permute-start(bf16[528,128]{1,0:T(8,128)(2,1)S(1)} %get-tuple-element.47), channel_id=1, source_target_pairs={{0,8},{4,12},{8,0},{12,4},{16,24},{20,28},{24,16},{28,20},{1,9},{5... | collective-permute-start | bytes 405512 | tf_op jit(solution)/shard_map/ppermute | solution.py:21
  47.6 7.2 %collective-permute-start.12 = (bf16[200,128]{1,0:T(8,128)(2,1)S(1)}, bf16[200,128]{1,0:T(8,128)(2,1)S(1)}, u32[]{:S(2)}, u32[]{:S(2)}) collective-permute-start(bf16[200,128]{1,0:T(8,128)(2,1)S(1)} %get-tuple-element.45), channel_id=1, source_target_pairs={{0,28},{4,24},{8,20},{12,16},{16,12},{20,8},{24,4},{28,0},{1,29},{... | collective-permute-start | bytes 153608 | tf_op jit(solution)/shard_map/ppermute | solution.py:21
  51.1 5.9 %collective-permute-start.13 = (bf16[200,128]{1,0:T(8,128)(2,1)S(1)}, bf16[200,128]{1,0:T(8,128)(2,1)S(1)}, u32[]{:S(2)}, u32[]{:S(2)}) collective-permute-start(bf16[200,128]{1,0:T(8,128)(2,1)S(1)} %get-tuple-element.46), channel_id=1, source_target_pairs={{0,24},{4,28},{8,16},{12,20},{16,8},{20,12},{24,0},{28,4},{1,25},{... | collective-permute-start | bytes 153608 | tf_op jit(solution)/shard_map/ppermute | solution.py:21

commit v4 on v3

--- a/solution.py
+++ b/solution.py
@@ -12,7 +12,6 @@
 KINDS = 6
 MIB = 1 << 20
 WHOLE = pl.BlockSpec(memory_space=pltpu.VMEM)
-SCALARS = pl.BlockSpec(memory_space=pltpu.SMEM)
 FAR = pl.BlockSpec(memory_space=pltpu.HBM)
 
 
@@ -218,10 +217,8 @@
         return index
     per_slab = group // slabs
     block = (slab ^ (index // per_slab)) * per_slab + index % per_slab
-    place = 0
-    for section in range(group):
-        place = jnp.where(sub_map[section] == block, section, place)
-    return place
+    number = lax.broadcasted_iota(jnp.int32, sub_map.shape, 1).astype(jnp.float32)
+    return jnp.sum(jnp.where(sub_map[...] == block, number, 0.0)).astype(jnp.int32)
 
 
 def form_rows(group, pulse_count, sources, first, sub_map, blocks, steering, image):
@@ -521,7 +518,7 @@
 
     bands, waves = tables(early, masks, group, rows + 8, [early_pack, *mine, *theirs])
 
-    cut_row = -(-rows * 5 // 8 // 16) * 16
+    cut_row = -(-rows // 2 // 16) * 16
     bounds = ((0, cut_row), (cut_row, rows - cut_row))
     pieces = [4 * count + 8 for _, count in bounds]
     upper_order, lower_order = send_order(group)
@@ -547,13 +544,13 @@
                 len(blocks),
             ),
             out_shape=[jax.ShapeDtypeStruct((size, half), jnp.bfloat16) for size in sizes],
-            in_specs=[SCALARS] + [WHOLE] * (len(blocks) + 3 + len(arrays)),
+            in_specs=[WHOLE] * (len(blocks) + 4 + len(arrays)),
             out_specs=[WHOLE] * group,
             scratch_shapes=scratch
             + [pltpu.VMEM((group, 2, 2, count + 16, half), jnp.float32)] * (segments - 1),
             compiler_params=params(10),
             cost_estimate=cost(4_000_000_000),
-        )(sub_map, *blocks, steering, bands, waves, *arrays)
+        )(sub_map[None], *blocks, steering, bands, waves, *arrays)
 
     arrived = {}
 

time: 58.4 us -> 56.7 us (0.971)
  the two profiles are of different devices: /device:TPU:4 before, /device:TPU:1 now
where the time goes in v4:
time: 56.7 us; the launch traced here: 56.1 us
  starting transfers between devices  32.7 us (58%)
  Pallas kernels  12.9 us (23%)
  waiting for transfers between devices  10.2 us (18%)
    ppermute x15, starting transfers between devices, exchanged(): lax.ppermute(block, axis, [(source, source ^ mask) for source in range(co...  20.2 us
    ppermute x15, waiting for transfers between devices, exchanged(): lax.ppermute(block, axis, [(source, source ^ mask) for source in range(co...  10.2 us
    ppermute x1, starting transfers between devices, on_device(): edge = lax.ppermute(edge_rows, ('sub', 'rng'), route)  6.74 us
    ppermute x4, starting transfers between devices, on_device(): mine.append(lax.ppermute(early_pack, ('sub', 'rng'), route))  5.78 us
    pallas_call x2, Pallas kernels, merge(): pl.pallas_call(functools.partial(merge_kernel, group, segments, chunk, fi...  4.2 us
    pallas_call x2, Pallas kernels, tables(): pl.pallas_call(functools.partial(table_kernel, group, terms, sources, tap...  3.98 us
    pallas_call x3, Pallas kernels, on_device(): pl.pallas_call(functools.partial(final_kernel, jobs, count, group, rows,...  3.32 us
    pallas_call x1, Pallas kernels, on_device(): pl.pallas_call(functools.partial(cut_kernel, slabs, segments, taps, half)...  1.42 us
  transfers between devices with their start and end apart: 20, of which 4 were waited for; matrix products, arithmetic and copies ran while one was open for 0% of the time, Pallas kernels for 18%

profile of v4, /device:TPU:1, one launch (start us, length us, event | category | flops | bytes accessed | tf_op | source)
XLA Modules:
  0.0 56.1 jit_solution(6473762909967165478)
XLA Ops:
  0.0 1.4 %cut.1 = (bf16[2,128,512]{2,1,0:T(8,128)(2,1)S(1)}, bf16[2,128,512]{2,1,0:T(8,128)(2,1)S(1)}, bf16[2,128,512]{2,1,0:T(8,128)(2,1)S(1)}, bf16[2,128,512]{2,1,0:T(...) custom-call(bf16[2,4,128,512]{3,2,1,0:T(8,128)(2,1)} %echoes.1, s32[1,3,2,256]{3,2,1,0:T(2,128)} %offset.1, ...), custom_call_target="tpu_custom_call" | custom-call | flops 1000000000 | bytes 1048576 | tf_op jit(solution)/shard_map/cut/pallas_call | solution.py:434
  1.5 4.2 %collective-permute-start.3 = (bf16[56,256]{1,0:T(8,128)(2,1)S(1)}, bf16[56,256]{1,0:T(8,128)(2,1)S(1)}, u32[]{:S(2)}, u32[]{:S(2)}) collective-permute-start(bf16[56,256]{1,0:T(8,128)(2,1)S(1)} %get-tuple-element.35.refs_0_), channel_id=1, source_target_pairs={{0,28},{1,25},{2,30},{3,27},{4,24},{5,29},{6,26},{7,31},{8,20},{9,... | collective-permute-start | bytes 86024 | tf_op jit(solution)/shard_map/ppermute | solution.py:459
  6.0 1.2 %collective-permute-start.6 = (bf16[56,256]{1,0:T(8,128)(2,1)S(1)}, bf16[56,256]{1,0:T(8,128)(2,1)S(1)}, u32[]{:S(2)}, u32[]{:S(2)}) collective-permute-start(bf16[56,256]{1,0:T(8,128)(2,1)S(1)} %get-tuple-element.35.refs_0_), channel_id=1, source_target_pairs={{0,4},{1,5},{2,6},{3,7},{4,0},{5,1},{6,2},{7,3},{8,12},{9,13},{10,... | collective-permute-start | bytes 86024 | tf_op jit(solution)/shard_map/ppermute | solution.py:459
  7.2 3.7 %collective-permute-start.2 = (bf16[2,128,512]{2,1,0:T(8,128)(2,1)S(1)}, bf16[2,128,512]{2,1,0:T(8,128)(2,1)S(1)}, u32[]{:S(2)}, u32[]{:S(2)}) collective-permute-start(bf16[2,128,512]{2,1,0:T(8,128)(2,1)S(1)} %get-tuple-element.34), channel_id=1, source_target_pairs={{0,3},{1,2},{2,1},{3,0},{4,7},{5,6},{6,5},{7,4},{8,11},{9,10},{10,... | collective-permute-start | bytes 786440 | tf_op jit(solution)/shard_map/ppermute | solution.py:20
  10.9 2.4 %collective-permute-start.8 = (bf16[56,256]{1,0:T(8,128)(2,1)S(1)}, bf16[56,256]{1,0:T(8,128)(2,1)S(1)}, u32[]{:S(2)}, u32[]{:S(2)}) collective-permute-start(bf16[56,256]{1,0:T(8,128)(2,1)S(1)} %collective-permute-done.4.refs_2_), channel_id=1, source_target_pairs={{0,1},{1,0},{2,3},{3,2},{4,5},{5,4},{6,7},{7,6},{8,9},{9,8},{10,11... | collective-permute-start | bytes 86024 | tf_op jit(solution)/shard_map/ppermute | solution.py:20
  13.3 0.5 collective-permute-start
  13.8 1.2 %collective-permute-start.1 = (bf16[2,128,512]{2,1,0:T(8,128)(2,1)S(1)}, bf16[2,128,512]{2,1,0:T(8,128)(2,1)S(1)}, u32[]{:S(2)}, u32[]{:S(2)}) collective-permute-start(bf16[2,128,512]{2,1,0:T(8,128)(2,1)S(1)} %get-tuple-element.33), channel_id=1, source_target_pairs={{0,2},{1,3},{2,0},{3,1},{4,6},{5,7},{6,4},{7,5},{8,10},{9,11},{10,... | collective-permute-start | bytes 786440 | tf_op jit(solution)/shard_map/ppermute | solution.py:20
  15.1 2.7 %shard_map.73 = (bf16[8,4,256,256]{3,2,1,0:T(8,128)(2,1)S(1)}, f32[8,4,2,136,256]{4,3,2,1,0:T(8,128)S(1)}) custom-call(bf16[56,256]{1,0:T(8,128)(2,1)S(1)} %get-tuple-element.35.refs_0_, bf16[56,256]{1,0:T(8,128)(2,1)S(1)} %collective-permute-done.3.refs_1_, bf16[56,256]{1,0:T(8,128)(2,1)S(1)} %collective-permute-done.4.refs_2_, ...), custom_call_target="tpu_custom_call" | custom-call | flops 2000000000 | bytes 1048576 | tf_op jit(solution)/shard_map/pallas_call | solution.py:491
  17.8 5.5 %collective-permute-done.1.refs_2_ = bf16[2,128,512]{2,1,0:T(8,128)(2,1)S(1)} collective-permute-done((bf16[2,128,512]{2,1,0:T(8,128)(2,1)S(1)}, bf16[2,128,512]{2,1,0:T(8,128)(2,1)S(1)}, u32[]{:S(2)}, u32[]{:S(2)}) %collective-permute-start.1) | collective-permute-done | bytes 262176 | tf_op jit(solution)/shard_map/ppermute | solution.py:20
  23.3 6.7 %collective-permute-start.10 = (bf16[4,2,8,512]{3,2,1,0:T(8,128)(2,1)S(1)}, bf16[4,2,8,512]{3,2,1,0:T(8,128)(2,1)S(1)}, u32[]{:S(2)}, u32[]{:S(2)}) collective-permute-start(bf16[4,2,8,512]{3,2,1,0:T(8,128)(2,1)S(1)} %pad_maximum_fusion), channel_id=1, source_target_pairs={{1,28},{2,29},{3,30},{4,0},{5,1},{6,2},{7,3},{8,4},{9,5},{10,6},{1... | collective-permute-start | bytes 196616 | tf_op jit(solution)/shard_map/ppermute | solution.py:488
  30.1 2.1 %shard_map.74 = (bf16[264,128]{1,0:T(8,128)(2,1)S(1)}, bf16[264,128]{1,0:T(8,128)(2,1)S(1)}, bf16[264,128]{1,0:T(8,128)(2,1)S(1)}, bf16[264,128]{1,0:T(8,128)(2,...) custom-call(s32[1,8]{1,0:T(1,128)S(1)} %bitcast.9, ...), custom_call_target="tpu_custom_call" | custom-call | flops 4000000000 | bytes 1048576 | tf_op jit(solution)/shard_map/pallas_call | solution.py:534
  32.4 2.1 %shard_map.75 = (bf16[528,128]{1,0:T(8,128)(2,1)S(1)}, bf16[528,128]{1,0:T(8,128)(2,1)S(1)}, bf16[528,128]{1,0:T(8,128)(2,1)S(1)}, bf16[528,128]{1,0:T(8,128)(2,...) custom-call(s32[1,8]{1,0:T(1,128)S(1)} %bitcast.10, ...), custom_call_target="tpu_custom_call" | custom-call | flops 4000000000 | bytes 1048576 | tf_op jit(solution)/shard_map/pallas_call | solution.py:534
  34.7 4.3 %collective-permute-start.16 = (bf16[528,128]{1,0:T(8,128)(2,1)S(1)}, bf16[528,128]{1,0:T(8,128)(2,1)S(1)}, u32[]{:S(2)}, u32[]{:S(2)}) collective-permute-start(bf16[528,128]{1,0:T(8,128)(2,1)S(1)} %get-tuple-element.52), channel_id=1, source_target_pairs={{0,12},{4,8},{8,4},{12,0},{16,28},{20,24},{24,20},{28,16},{1,13},{... | collective-permute-start | bytes 405512 | tf_op jit(solution)/shard_map/ppermute | solution.py:20
  39.0 1.7 %collective-permute-start.17 = (bf16[528,128]{1,0:T(8,128)(2,1)S(1)}, bf16[528,128]{1,0:T(8,128)(2,1)S(1)}, u32[]{:S(2)}, u32[]{:S(2)}) collective-permute-start(bf16[528,128]{1,0:T(8,128)(2,1)S(1)} %get-tuple-element.53), channel_id=1, source_target_pairs={{0,4},{4,0},{8,12},{12,8},{16,20},{20,16},{24,28},{28,24},{1,5},{5... | collective-permute-start | bytes 405512 | tf_op jit(solution)/shard_map/ppermute | solution.py:20
  40.7 1.3 %shard_map.76 = (bf16[1,2,256,256]{3,2,1,0:T(8,128)(2,1)S(1)}, f32[8,2,2,128,256]{4,3,2,1,0:T(8,128)S(1)}) custom-call(bf16[32,256]{1,0:T(8,128)(2,1)S(1)} %get-tuple-element.48.refs_0_), custom_call_target="tpu_custom_call" | custom-call | flops 2000000000 | bytes 1048576 | tf_op jit(solution)/shard_map/pallas_call | solution.py:491
  42.3 2.6 %collective-permute-start.14 = (bf16[528,128]{1,0:T(8,128)(2,1)S(1)}, bf16[528,128]{1,0:T(8,128)(2,1)S(1)}, u32[]{:S(2)}, u32[]{:S(2)}) collective-permute-start(bf16[528,128]{1,0:T(8,128)(2,1)S(1)} %get-tuple-element.47), channel_id=1, source_target_pairs={{0,8},{4,12},{8,0},{12,4},{16,24},{20,28},{24,16},{28,20},{1,9},{5... | collective-permute-start | bytes 405512 | tf_op jit(solution)/shard_map/ppermute | solution.py:20
  45.0 1.0 %final.3.refs_5_ = bf16[2,1024,256]{2,1,0:T(8,128)(2,1)} custom-call(bf16[528,128]{1,0:T(8,128)(2,1)S(1)} %get-tuple-element.54.refs_0_, bf16[264,128]{1,0:T(8,128)(2,1)S(1)} %collective-permute-done.18.refs_1_, bf16[264,128]{1,0:T(8,128)(2,1)S(1)} %collective-permute-done.19.refs_2_, bf16[1,2,256,256]{3,2,1,0:T(8,128)(2,1)S(1)} %get-tuple-element.49.refs_3_.refs_4_, ...), custom_call_target="tpu_custom_call" | custom-call | flops 1000000000 | bytes 1048576 | tf_op jit(solution)/shard_map/final/pallas_call | solution.py:586
  46.0 1.1 %collective-permute-start.12 = (bf16[264,128]{1,0:T(8,128)(2,1)S(1)}, bf16[264,128]{1,0:T(8,128)(2,1)S(1)}, u32[]{:S(2)}, u32[]{:S(2)}) collective-permute-start(bf16[264,128]{1,0:T(8,128)(2,1)S(1)} %get-tuple-element.45), channel_id=1, source_target_pairs={{0,28},{4,24},{8,20},{12,16},{16,12},{20,8},{24,4},{28,0},{1,29},{... | collective-permute-start | bytes 202760 | tf_op jit(solution)/shard_map/ppermute | solution.py:20
  47.1 1.9 %collective-permute-start.13 = (bf16[264,128]{1,0:T(8,128)(2,1)S(1)}, bf16[264,128]{1,0:T(8,128)(2,1)S(1)}, u32[]{:S(2)}, u32[]{:S(2)}) collective-permute-start(bf16[264,128]{1,0:T(8,128)(2,1)S(1)} %get-tuple-element.46), channel_id=1, source_target_pairs={{0,24},{4,28},{8,16},{12,20},{16,8},{20,12},{24,0},{28,4},{1,25},{... | collective-permute-start | bytes 202760 | tf_op jit(solution)/shard_map/ppermute | solution.py:20
  49.1 1.2 %final.4.refs_6_ = bf16[2,1024,256]{2,1,0:T(8,128)(2,1)} custom-call(bf16[528,128]{1,0:T(8,128)(2,1)S(1)} %collective-permute-done.15.refs_0_, bf16[528,128]{1,0:T(8,128)(2,1)S(1)} %collective-permute-done.16.refs_1_, bf16[528,128]{1,0:T(8,128)(2,1)S(1)} %collective-permute-done.17.refs_2_, ...), custom_call_target="tpu_custom_call", output_to_operand_aliasing={{}: (5, {})} | custom-call | flops 1000000000 | bytes 1048576 | tf_op jit(solution)/shard_map/final/pallas_call | solution.py:586
  50.2 3.4 %collective-permute-done.12.refs_1_ = bf16[264,128]{1,0:T(8,128)(2,1)S(1)} collective-permute-done((bf16[264,128]{1,0:T(8,128)(2,1)S(1)}, bf16[264,128]{1,0:T(8,128)(2,1)S(1)}, u32[]{:S(2)}, u32[]{:S(2)}) %collective-permute-start.12) | collective-permute-done | bytes 67616 | tf_op jit(solution)/shard_map/ppermute | solution.py:20
  53.6 0.4 collective-permute-done.13.refs_2_
  54.0 0.9 %collective-permute-done.14.refs_3_ = bf16[528,128]{1,0:T(8,128)(2,1)S(1)} collective-permute-done((bf16[528,128]{1,0:T(8,128)(2,1)S(1)}, bf16[528,128]{1,0:T(8,128)(2,1)S(1)}, u32[]{:S(2)}, u32[]{:S(2)}) %collective-permute-start.14) | collective-permute-done | bytes 135200 | tf_op jit(solution)/shard_map/ppermute | solution.py:20
  55.0 1.1 %final.5 = bf16[2,1024,256]{2,1,0:T(8,128)(2,1)} custom-call(bf16[528,128]{1,0:T(8,128)(2,1)S(1)} %collective-permute-done.11.refs_0_, bf16[264,128]{1,0:T(8,128)(2,1)S(1)} %collective-permute-done.12.refs_1_, bf16[264,128]{1,0:T(8,128)(2,1)S(1)} %collective-permute-done.13.refs_2_, ...), custom_call_target="tpu_custom_call", output_to_operand_aliasing={{}: (6, {})} | custom-call | flops 1000000000 | bytes 1048576 | tf_op jit(solution)/shard_map/final/pallas_call | solution.py:586
  (33 shorter events, 1.2 us)
Async XLA Ops:
  1.4 28.6 %copy-start = (bf16[2,256,256]{2,1,0:T(8,128)(2,1)S(1)}, bf16[2,256,256]{2,1,0:T(8,128)(2,1)}, u32[]{:S(2)}) copy-start(bf16[2,256,256]{2,1,0:T(8,128)(2,1)} %refs_4_.3) | copy-start | bytes 786436
  1.4 28.6 %copy-start.1 = (s32[8]{0:T(128)S(1)}, s32[8]{0:T(128)}, u32[]{:S(2)}) copy-start(s32[8]{0:T(128)} %param.9) | copy-start | bytes 100
  1.5 9.4 %collective-permute-start.3 = (bf16[56,256]{1,0:T(8,128)(2,1)S(1)}, bf16[56,256]{1,0:T(8,128)(2,1)S(1)}, u32[]{:S(2)}, u32[]{:S(2)}) collective-permute-start(bf16[56,256]{1,0:T(8,128)(2,1)S(1)} %get-tuple-element.35.refs_0_), channel_id=1, source_target_pairs={{0,28},{1,25},{2,30},{3,27},{4,24},{5,29},{6,26},{7,31},{8,20},{9,... | collective-permute-start | bytes 86024 | tf_op jit(solution)/shard_map/ppermute | solution.py:459
  5.7 5.2 %collective-permute-start.4 = (bf16[56,256]{1,0:T(8,128)(2,1)S(1)}, bf16[56,256]{1,0:T(8,128)(2,1)S(1)}, u32[]{:S(2)}, u32[]{:S(2)}) collective-permute-start(bf16[56,256]{1,0:T(8,128)(2,1)S(1)} %get-tuple-element.35.refs_0_), channel_id=1, source_target_pairs={{0,20},{1,17},{2,22},{3,19},{4,16},{5,21},{6,18},{7,23},{8,28},{9,... | collective-permute-start | bytes 86024 | tf_op jit(solution)/shard_map/ppermute | solution.py:459
  5.7 7.7 %collective-permute-start.5 = (bf16[56,256]{1,0:T(8,128)(2,1)S(1)}, bf16[56,256]{1,0:T(8,128)(2,1)S(1)}, u32[]{:S(2)}, u32[]{:S(2)}) collective-permute-start(bf16[56,256]{1,0:T(8,128)(2,1)S(1)} %get-tuple-element.35.refs_0_), channel_id=1, source_target_pairs={{0,12},{1,9},{2,14},{3,11},{4,8},{5,13},{6,10},{7,15},{8,4},{9,1},... | collective-permute-start | bytes 86024 | tf_op jit(solution)/shard_map/ppermute | solution.py:459
  6.0 7.3 %collective-permute-start.6 = (bf16[56,256]{1,0:T(8,128)(2,1)S(1)}, bf16[56,256]{1,0:T(8,128)(2,1)S(1)}, u32[]{:S(2)}, u32[]{:S(2)}) collective-permute-start(bf16[56,256]{1,0:T(8,128)(2,1)S(1)} %get-tuple-element.35.refs_0_), channel_id=1, source_target_pairs={{0,4},{1,5},{2,6},{3,7},{4,0},{5,1},{6,2},{7,3},{8,12},{9,13},{10,... | collective-permute-start | bytes 86024 | tf_op jit(solution)/shard_map/ppermute | solution.py:459
  7.2 10.6 %collective-permute-start.2 = (bf16[2,128,512]{2,1,0:T(8,128)(2,1)S(1)}, bf16[2,128,512]{2,1,0:T(8,128)(2,1)S(1)}, u32[]{:S(2)}, u32[]{:S(2)}) collective-permute-start(bf16[2,128,512]{2,1,0:T(8,128)(2,1)S(1)} %get-tuple-element.34), channel_id=1, source_target_pairs={{0,3},{1,2},{2,1},{3,0},{4,7},{5,6},{6,5},{7,4},{8,11},{9,10},{10,... | collective-permute-start | bytes 786440 | tf_op jit(solution)/shard_map/ppermute | solution.py:20
  10.9 2.9 %collective-permute-start.7 = (bf16[56,256]{1,0:T(8,128)(2,1)S(1)}, bf16[56,256]{1,0:T(8,128)(2,1)S(1)}, u32[]{:S(2)}, u32[]{:S(2)}) collective-permute-start(bf16[56,256]{1,0:T(8,128)(2,1)S(1)} %collective-permute-done.3.refs_1_), channel_id=1, source_target_pairs={{0,1},{1,0},{2,3},{3,2},{4,5},{5,4},{6,7},{7,6},{8,9},{9,8},{10,11... | collective-permute-start | bytes 86024 | tf_op jit(solution)/shard_map/ppermute | solution.py:20
  10.9 4.2 %collective-permute-start.8 = (bf16[56,256]{1,0:T(8,128)(2,1)S(1)}, bf16[56,256]{1,0:T(8,128)(2,1)S(1)}, u32[]{:S(2)}, u32[]{:S(2)}) collective-permute-start(bf16[56,256]{1,0:T(8,128)(2,1)S(1)} %collective-permute-done.4.refs_2_), channel_id=1, source_target_pairs={{0,1},{1,0},{2,3},{3,2},{4,5},{5,4},{6,7},{7,6},{8,9},{9,8},{10,11... | collective-permute-start | bytes 86024 | tf_op jit(solution)/shard_map/ppermute | solution.py:20
  13.3 1.8 %collective-permute-start.9 = (bf16[56,256]{1,0:T(8,128)(2,1)S(1)}, bf16[56,256]{1,0:T(8,128)(2,1)S(1)}, u32[]{:S(2)}, u32[]{:S(2)}) collective-permute-start(bf16[56,256]{1,0:T(8,128)(2,1)S(1)} %collective-permute-done.5.refs_3_), channel_id=1, source_target_pairs={{0,1},{1,0},{2,3},{3,2},{4,5},{5,4},{6,7},{7,6},{8,9},{9,8},{10,11... | collective-permute-start | bytes 86024 | tf_op jit(solution)/shard_map/ppermute | solution.py:20
  13.3 10.0 %collective-permute-start = (bf16[2,128,512]{2,1,0:T(8,128)(2,1)S(1)}, bf16[2,128,512]{2,1,0:T(8,128)(2,1)S(1)}, u32[]{:S(2)}, u32[]{:S(2)}) collective-permute-start(bf16[2,128,512]{2,1,0:T(8,128)(2,1)S(1)} %get-tuple-element.32), channel_id=1, source_target_pairs={{0,1},{1,0},{2,3},{3,2},{4,5},{5,4},{6,7},{7,6},{8,9},{9,8},{10,11... | collective-permute-start | bytes 786440 | tf_op jit(solution)/shard_map/ppermute | solution.py:20
  13.8 9.4 %collective-permute-start.1 = (bf16[2,128,512]{2,1,0:T(8,128)(2,1)S(1)}, bf16[2,128,512]{2,1,0:T(8,128)(2,1)S(1)}, u32[]{:S(2)}, u32[]{:S(2)}) collective-permute-start(bf16[2,128,512]{2,1,0:T(8,128)(2,1)S(1)} %get-tuple-element.33), channel_id=1, source_target_pairs={{0,2},{1,3},{2,0},{3,1},{4,6},{5,7},{6,4},{7,5},{8,10},{9,11},{10,... | collective-permute-start | bytes 786440 | tf_op jit(solution)/shard_map/ppermute | solution.py:20
  23.3 9.1 %collective-permute-start.10 = (bf16[4,2,8,512]{3,2,1,0:T(8,128)(2,1)S(1)}, bf16[4,2,8,512]{3,2,1,0:T(8,128)(2,1)S(1)}, u32[]{:S(2)}, u32[]{:S(2)}) collective-permute-start(bf16[4,2,8,512]{3,2,1,0:T(8,128)(2,1)S(1)} %pad_maximum_fusion), channel_id=1, source_target_pairs={{1,28},{2,29},{3,30},{4,0},{5,1},{6,2},{7,3},{8,4},{9,5},{10,6},{1... | collective-permute-start | bytes 196616 | tf_op jit(solution)/shard_map/ppermute | solution.py:488
  32.2 9.8 %collective-permute-start.18 = (bf16[264,128]{1,0:T(8,128)(2,1)S(1)}, bf16[264,128]{1,0:T(8,128)(2,1)S(1)}, u32[]{:S(2)}, u32[]{:S(2)}) collective-permute-start(bf16[264,128]{1,0:T(8,128)(2,1)S(1)} %get-tuple-element.55), channel_id=1, source_target_pairs={{0,28},{4,24},{8,20},{12,16},{16,12},{20,8},{24,4},{28,0},{1,29},{... | collective-permute-start | bytes 202760 | tf_op jit(solution)/shard_map/ppermute | solution.py:20
  32.3 10.0 %collective-permute-start.19 = (bf16[264,128]{1,0:T(8,128)(2,1)S(1)}, bf16[264,128]{1,0:T(8,128)(2,1)S(1)}, u32[]{:S(2)}, u32[]{:S(2)}) collective-permute-start(bf16[264,128]{1,0:T(8,128)(2,1)S(1)} %get-tuple-element.56), channel_id=1, source_target_pairs={{0,24},{4,28},{8,16},{12,20},{16,8},{20,12},{24,0},{28,4},{1,25},{... | collective-permute-start | bytes 202760 | tf_op jit(solution)/shard_map/ppermute | solution.py:20
  34.5 11.5 %collective-permute-start.15 = (bf16[528,128]{1,0:T(8,128)(2,1)S(1)}, bf16[528,128]{1,0:T(8,128)(2,1)S(1)}, u32[]{:S(2)}, u32[]{:S(2)}) collective-permute-start(bf16[528,128]{1,0:T(8,128)(2,1)S(1)} %get-tuple-element.51), channel_id=1, source_target_pairs={{0,20},{4,16},{8,28},{12,24},{16,4},{20,0},{24,12},{28,8},{1,21},{... | collective-permute-start | bytes 405512 | tf_op jit(solution)/shard_map/ppermute | solution.py:20
  34.7 12.4 %collective-permute-start.16 = (bf16[528,128]{1,0:T(8,128)(2,1)S(1)}, bf16[528,128]{1,0:T(8,128)(2,1)S(1)}, u32[]{:S(2)}, u32[]{:S(2)}) collective-permute-start(bf16[528,128]{1,0:T(8,128)(2,1)S(1)} %get-tuple-element.52), channel_id=1, source_target_pairs={{0,12},{4,8},{8,4},{12,0},{16,28},{20,24},{24,20},{28,16},{1,13},{... | collective-permute-start | bytes 405512 | tf_op jit(solution)/shard_map/ppermute | solution.py:20
  39.0 10.1 %collective-permute-start.17 = (bf16[528,128]{1,0:T(8,128)(2,1)S(1)}, bf16[528,128]{1,0:T(8,128)(2,1)S(1)}, u32[]{:S(2)}, u32[]{:S(2)}) collective-permute-start(bf16[528,128]{1,0:T(8,128)(2,1)S(1)} %get-tuple-element.53), channel_id=1, source_target_pairs={{0,4},{4,0},{8,12},{12,8},{16,20},{20,16},{24,28},{28,24},{1,5},{5... | collective-permute-start | bytes 405512 | tf_op jit(solution)/shard_map/ppermute | solution.py:20
  42.0 12.0 %collective-permute-start.11 = (bf16[528,128]{1,0:T(8,128)(2,1)S(1)}, bf16[528,128]{1,0:T(8,128)(2,1)S(1)}, u32[]{:S(2)}, u32[]{:S(2)}) collective-permute-start(bf16[528,128]{1,0:T(8,128)(2,1)S(1)} %get-tuple-element.44), channel_id=1, source_target_pairs={{0,16},{4,20},{8,24},{12,28},{16,0},{20,4},{24,8},{28,12},{1,17},{... | collective-permute-start | bytes 405512 | tf_op jit(solution)/shard_map/ppermute | solution.py:20
  42.3 12.6 %collective-permute-start.14 = (bf16[528,128]{1,0:T(8,128)(2,1)S(1)}, bf16[528,128]{1,0:T(8,128)(2,1)S(1)}, u32[]{:S(2)}, u32[]{:S(2)}) collective-permute-start(bf16[528,128]{1,0:T(8,128)(2,1)S(1)} %get-tuple-element.47), channel_id=1, source_target_pairs={{0,8},{4,12},{8,0},{12,4},{16,24},{20,28},{24,16},{28,20},{1,9},{5... | collective-permute-start | bytes 405512 | tf_op jit(solution)/shard_map/ppermute | solution.py:20
  46.0 7.6 %collective-permute-start.12 = (bf16[264,128]{1,0:T(8,128)(2,1)S(1)}, bf16[264,128]{1,0:T(8,128)(2,1)S(1)}, u32[]{:S(2)}, u32[]{:S(2)}) collective-permute-start(bf16[264,128]{1,0:T(8,128)(2,1)S(1)} %get-tuple-element.45), channel_id=1, source_target_pairs={{0,28},{4,24},{8,20},{12,16},{16,12},{20,8},{24,4},{28,0},{1,29},{... | collective-permute-start | bytes 202760 | tf_op jit(solution)/shard_map/ppermute | solution.py:20
  47.1 6.9 %collective-permute-start.13 = (bf16[264,128]{1,0:T(8,128)(2,1)S(1)}, bf16[264,128]{1,0:T(8,128)(2,1)S(1)}, u32[]{:S(2)}, u32[]{:S(2)}) collective-permute-start(bf16[264,128]{1,0:T(8,128)(2,1)S(1)} %get-tuple-element.46), channel_id=1, source_target_pairs={{0,24},{4,28},{8,16},{12,20},{16,8},{20,12},{24,0},{28,4},{1,25},{... | collective-permute-start | bytes 202760 | tf_op jit(solution)/shard_map/ppermute | solution.py:20
